TPU v7x, 32 devices: a whole 2x2x4 slice. The times are simulated.
32 devices in a mesh: grp: 2 (over y), ctx: 4 (over z), hd: 4 (over x, core).
Axes of the slice: x: 2, y: 2, z: 4, core: 2. Of those that a mesh axis runs over, the one named last changes fastest.
Arguments:
- query: bfloat16 [1024, 4096], P(('grp', 'ctx'), 'hd'), parts along dimension 0, may hold values from -6 to 6
- keys: bfloat16 [1024, 1024], P(('grp', 'ctx'), 'hd'), parts along dimension 0, may hold values from -6 to 6
- values: bfloat16 [1024, 1024], P(('grp', 'ctx'), 'hd'), parts along dimension 0, may hold values from -6 to 6
- m_x: bfloat16 [1024, 8192], P(('grp', 'ctx'), 'hd'), parts along dimension 0, may hold values from -6 to 6
- m_z: bfloat16 [1024, 8192], P(('grp', 'ctx'), 'hd'), parts along dimension 0, may hold values from -6 to 6
- m_b: bfloat16 [1024, 1024], P(('grp', 'ctx'), 'hd'), parts along dimension 0, may hold values from -6 to 6
- m_c: bfloat16 [1024, 1024], P(('grp', 'ctx'), 'hd'), parts along dimension 0, may hold values from -0.5 to 0.5
- dt_raw: bfloat16 [1024, 128], P(('grp', 'ctx'), 'hd'), parts along dimension 0, may hold values from -5 to 25
- dt_bias: float32 [128], P('hd'), may hold values from -0.5 to 0.5
- a_log: float32 [128], P('hd'), may hold values from -10 to 0
- d_skip: float32 [128], P('hd'), may hold values from 0.5 to 2
- norm_gain: float32 [8192], P('hd'), may hold values from 0.5 to 1.5
Outputs:
- context: bfloat16 [1024, 4096], P(('grp', 'ctx'), 'hd'), parts along dimension 0
- mixed: bfloat16 [1024, 8192], P(('grp', 'ctx'), 'hd'), parts along dimension 0
There are 2 independent parts, one for each index of `grp`. A program takes and returns all parts, laid end to end along the dimension named above; an argument that names none is the same for every part. Nothing has to cross between parts.
All inputs are finite; a program needn't handle non-finite values.
Results may differ from a plain program's by a relative error of at most 0.009.
Values may be sent and summed in bfloat16 or wider, within the bound.
A program may use at most 64 MiB of HBM per device.

v0:
```python
import functools
import math

import jax
import jax.numpy as jnp
from jax import lax
from jax.experimental import pallas as pl
from jax.experimental.pallas import tpu as pltpu
from jax.sharding import PartitionSpec as P

HEAD_SIZE = 128
MP = 64
MN = 128
NORM_EPS = 1e-05
MASKED = -1e30
HIGHEST = lax.Precision.HIGHEST
F32 = jnp.float32
BF16 = jnp.bfloat16
INPUT_SPACE = pltpu.HBM
HOP_SLOTS = 3
PIECE = 256


def dot(a, b, ca=1, cb=0, precision=None):
    return lax.dot_general(
        a, b, (((ca,), (cb,)), ((), ())), preferred_element_type=F32, precision=precision
    )


def kernel(
    n, q_in, k_ref, v_ref, x_in, z_in, b_in, c_in, dt_in, bias_in, alog_in, skip_in,
    gain_in, ctx_out, mix_out,
    q_ref, x_ref, z_ref, b_ref, c_ref, dt_ref, bias_ref, alog_ref, skip_ref, gain_ref,
    k_all, v_all, bias_scr, ctx_stage, arrived, gated, base_scr, er_scr, xdt_scr, hs, runt, gmask,
    buf_a, buf_b, out_a, out_b, sloc_a, sloc_b, tot_a, tot_b,
    k_send, k_recv, v_send, v_recv, a_send, a_recv, b_send, b_recv, o_send, o_recv, load_sem,
):
    me = lax.axis_index("ctx")
    tok = q_ref.shape[0]
    half = tok // 2
    heads = dt_ref.shape[0]
    width = x_ref.shape[1]
    groups = b_ref.shape[1] // MN
    group_width = width // groups
    pieces, _, piece = buf_a.shape
    per_piece = piece // MP
    per_group = group_width // piece
    q_heads = q_ref.shape[1] // HEAD_SIZE
    repeat = q_ref.shape[1] // k_ref.shape[1]
    mesh_id = pl.DeviceIdType.MESH

    loads = [
        pltpu.make_async_copy(src, dst, load_sem.at[i])
        for i, (src, dst) in enumerate(
            (
                (dt_in, dt_ref), (bias_in, bias_ref), (alog_in, alog_ref), (skip_in, skip_ref),
                (b_in, b_ref), (c_in, c_ref), (x_in, x_ref), (gain_in, gain_ref), (z_in, z_ref),
                (k_ref, k_all.at[me]), (v_ref, v_all.at[me]), (q_in, q_ref),
            )
        )
    ]
    for load in loads:
        load.start()

    barrier = pltpu.get_barrier_semaphore()

    def greet(d, _):
        peer = lax.rem(me + d, n)
        pl.semaphore_signal(barrier, inc=1, device_id={"ctx": peer}, device_id_type=mesh_id)
        return 0

    lax.fori_loop(1, n, greet, 0)
    pl.semaphore_wait(barrier, n - 1)

    def remote(src, dst, send, recv, peer):
        return pltpu.make_async_remote_copy(
            src_ref=src, dst_ref=dst, send_sem=send, recv_sem=recv,
            device_id={"ctx": peer}, device_id_type=mesh_id,
        )

    def kv_copies(slot, sem_slot, peer, rows):
        return (
            remote(k_ref.at[rows], k_all.at[slot, rows], k_send.at[sem_slot], k_recv.at[slot], peer),
            remote(v_ref.at[rows], v_all.at[slot, rows], v_send.at[sem_slot], v_recv.at[slot], peer),
        )

    first = pl.ds(0, half)
    both = pl.ds(0, tok)

    def start_kv(d, _):
        @pl.when(me + d < n)
        def _():
            for copy in kv_copies(me, me + d, me + d, first):
                copy.start()

        @pl.when(me - d >= 0)
        def _():
            for copy in kv_copies(me, me - d, me - d, both):
                copy.start()

        return 0

    lax.fori_loop(1, n, start_kv, 0)

    row = lax.broadcasted_iota(jnp.int32, (tok, tok), 0)
    col = lax.broadcasted_iota(jnp.int32, (tok, tok), 1)
    for load in loads[:4]:
        load.wait()
    raw = dot((row == col).astype(BF16), dt_ref[...], 1, 1) + bias_ref[...]
    steps = jnp.maximum(raw, 0.0) + jnp.log1p(jnp.exp(-jnp.abs(raw)))
    decay = -steps * jnp.exp(alog_ref[...])
    lower = (col <= row) & ((row < half) == (col < half))
    tri = lower.astype(F32)
    hs[0:tok, :] = dot(tri, decay, precision=HIGHEST)
    hs[tok : 2 * tok, :] = steps
    hs[2 * tok :, :] = jnp.broadcast_to(skip_ref[...], (8, heads))
    runt[...] = dot(decay, tri, 0, 1, precision=HIGHEST)
    for load in loads[4:6]:
        load.wait()
    for g in range(groups):
        cols = slice(g * MN, (g + 1) * MN)
        gmask[g] = jnp.where(lower, dot(c_ref[:, cols], b_ref[:, cols], 1, 1), 0.0)

    @pl.when(me == 0)
    def _():
        buf_a[...] = jnp.zeros_like(buf_a)

    lane_head = lax.broadcasted_iota(jnp.int32, (heads, piece), 1) // MP
    head_row = lax.broadcasted_iota(jnp.int32, (heads, piece), 0)
    wide_head = lax.broadcasted_iota(jnp.int32, (heads, per_piece * tok), 1) // tok
    wide_row = lax.broadcasted_iota(jnp.int32, (heads, per_piece * tok), 0)
    left = lax.broadcasted_iota(jnp.int32, (tok, 2 * MP), 1) < MP

    def place(src, dst_of, kind, block_id, which):
        owner = block_id // 2
        slot = lax.rem(block_id, 2)

        @pl.when(owner == me)
        def _():
            pltpu.make_async_copy(src, dst_of(slot), o_recv.at[kind, slot]).start()

        @pl.when(owner != me)
        def _():
            remote(src, dst_of(slot), o_send.at[kind, which], o_recv.at[kind, slot], owner).start()

    def block_id(which):
        return me if which == 0 else 2 * n - 1 - me

    def send_piece(k, which):
        cols = pl.ds(pl.multiple_of(k * piece, piece), piece)
        place(
            gated.at[pl.ds(which * half, half), cols],
            lambda slot: arrived.at[pl.ds(pl.multiple_of(slot * half, half), half), cols],
            k, block_id(which), which,
        )

    def silu(value):
        return value / (1.0 + jnp.exp(-value))

    def prepare(k):
        cols = pl.ds(pl.multiple_of(k * piece, piece), piece)
        gcols = pl.ds(pl.multiple_of((k // per_group) * MN, MN), MN)
        pick = (head_row == k * per_piece + lane_head).astype(F32)
        spread = dot(hs[...], pick, precision=HIGHEST)
        run, step, skip = spread[0:tok], spread[tok : 2 * tok], spread[2 * tok : 2 * tok + 1]
        xs = x_ref[:, cols].astype(F32)
        xdt = xs * step
        last_a, last_b = run[half - 1 : half], run[tok - 1 : tok]
        b_rows = b_ref[:, gcols]
        sloc_a[k] = dot(b_rows[0:half], (xdt[0:half] * jnp.exp(last_a - run[0:half])).astype(BF16), 0, 0)
        sloc_b[k] = dot(b_rows[half:], (xdt[half:] * jnp.exp(last_b - run[half:])).astype(BF16), 0, 0)
        tot_a[k] = jnp.broadcast_to(jnp.exp(last_a), (8, piece))
        tot_b[k] = jnp.broadcast_to(jnp.exp(last_b), (8, piece))
        er_scr[:, cols] = jnp.exp(run)
        xdt_scr[:, cols] = xdt.astype(BF16)
        base_scr[:, cols] = skip * xs

    def within_blocks(k, _):
        cols = pl.ds(pl.multiple_of(k * piece, piece), piece)
        wide = dot(hs[0:tok, :], (wide_row == k * per_piece + wide_head).astype(F32), precision=HIGHEST)
        gm = gmask[k // per_group]
        inner = []
        for pair in range(per_piece // 2):
            weights = []
            for which in range(2):
                h = 2 * pair + which
                gap = wide[:, h * tok : (h + 1) * tok] - runt[pl.ds(k * per_piece + h, 1), :]
                weights.append((jnp.exp(jnp.minimum(gap, 0.0)) * gm).astype(BF16))
            at = pl.ds(pl.multiple_of(k * piece + pair * 2 * MP, 2 * MP), 2 * MP)
            part = xdt_scr[:, at]
            none = jnp.zeros_like(part)
            stacked = jnp.concatenate([jnp.where(left, part, none), jnp.where(left, none, part)], axis=0)
            inner.append(dot(jnp.concatenate(weights, axis=1), stacked))
        base_scr[:, cols] = base_scr[:, cols] + jnp.concatenate(inner, axis=1)
        return 0

    def gate(k, which, buffer):
        cols = pl.ds(pl.multiple_of(k * piece, piece), piece)
        gcols = pl.ds(pl.multiple_of((k // per_group) * MN, MN), MN)
        rows = slice(which * half, (which + 1) * half)
        carried = dot(c_ref[rows, gcols], buffer[k]) * er_scr[rows, cols]
        z = z_ref[rows, cols].astype(F32)
        gated[rows, cols] = ((base_scr[rows, cols] + carried) * silu(z)).astype(BF16)
        send_piece(k, which)

    def gate_a(k, _):
        gate(k, 0, buf_a)
        return 0

    def step_a(k):
        @pl.when(me == 0)
        def _():
            prepare(k)

        @pl.when(me > 0)
        def _():
            remote(out_a.at[k], buf_a.at[k], a_send.at[k], a_recv.at[k], me).wait_recv()

        state = (buf_a[k].astype(F32) * tot_a[k][0:1] + sloc_a[k]).astype(BF16)

        @pl.when(me < n - 1)
        def _():
            out_a[k] = state
            remote(out_a.at[k], buf_a.at[k], a_send.at[k], a_recv.at[k], me + 1).start()

        @pl.when(me == n - 1)
        def _():
            buf_b[k] = state

    def step_b(k):
        @pl.when(me < n - 1)
        def _():
            remote(out_b.at[k], buf_b.at[k], b_send.at[k], b_recv.at[k], me).wait_recv()

        @pl.when(me > 0)
        def _():
            out_b[k] = (buf_b[k].astype(F32) * tot_b[k][0:1] + sloc_b[k]).astype(BF16)
            remote(out_b.at[k], buf_b.at[k], b_send.at[k], b_recv.at[k], me - 1).start()

        gate(k, 1, buf_b)

    def attention():
        def wait_kv(s, _):
            @pl.when(s < me)
            def _():
                for copy in kv_copies(s, s, me, first):
                    copy.wait_recv()
                k_all[s, half:, :] = jnp.zeros((half, k_ref.shape[1]), BF16)
                v_all[s, half:, :] = jnp.zeros((half, k_ref.shape[1]), BF16)

            @pl.when(s > me)
            def _():
                for copy in kv_copies(s, s, me, both):
                    copy.wait_recv()

            return 0

        lax.fori_loop(0, n, wait_kv, 0)
        for load in loads[9:]:
            load.wait()
        key = lax.broadcasted_iota(jnp.int32, (tok, n * tok), 1)
        source = key // tok
        within = key - source * tok
        key_pos = jnp.where(
            within < half, source * half + within, (2 * n - 2 - source) * half + within
        )
        query = lax.broadcasted_iota(jnp.int32, (tok, n * tok), 0)
        query_pos = jnp.where(query < half, me * half + query, (2 * n - 2 - me) * half + query)
        bias_scr[...] = jnp.where(key_pos <= query_pos, 0.0, MASKED)
        scale = 1.0 / math.sqrt(HEAD_SIZE)

        def one_head(h, _):
            hcols = pl.ds(pl.multiple_of(h * HEAD_SIZE, HEAD_SIZE), HEAD_SIZE)
            kcols = pl.ds(pl.multiple_of((h // repeat) * HEAD_SIZE, HEAD_SIZE), HEAD_SIZE)
            keys = k_all[:, :, kcols].reshape(n * tok, HEAD_SIZE)
            values = v_all[:, :, kcols].reshape(n * tok, HEAD_SIZE)
            scores = dot(q_ref[:, hcols], keys, 1, 1) * scale + bias_scr[...]
            expo = jnp.exp(scores - jnp.max(scores, axis=-1, keepdims=True))
            total = jnp.sum(expo, axis=-1, keepdims=True)
            ctx_stage[:, hcols] = (dot(expo.astype(BF16), values) / total).astype(BF16)
            return 0

        lax.fori_loop(0, q_heads, one_head, 0)
        for which in range(2):
            place(
                ctx_stage.at[pl.ds(which * half, half)],
                lambda slot: ctx_out.at[pl.ds(pl.multiple_of(slot * half, half), half)],
                pieces, block_id(which), which,
            )

    for load in loads[6:9]:
        load.wait()
    lag = 2 * (n - 1) * HOP_SLOTS
    last = pieces + lag
    b_start = lag - me * HOP_SLOTS
    idle_between = me * HOP_SLOTS + pieces <= b_start
    attend_at = jnp.where(idle_between, b_start, last)

    def prepare_early(k, _):
        prepare(k)
        return 0

    @pl.when(me > 0)
    def _():
        lax.fori_loop(0, pieces, prepare_early, 0)

    inner_at = jnp.where(idle_between, b_start, 0)

    def slot_step(t, _):
        k_a = t - me * HOP_SLOTS
        k_b = t - (lag - me * HOP_SLOTS)

        @pl.when(t == inner_at)
        def _():
            lax.fori_loop(0, pieces, within_blocks, 0)

        @pl.when((k_a >= 0) & (k_a < pieces))
        def _():
            step_a(k_a)

        @pl.when(t == attend_at)
        def _():
            attention()
            lax.fori_loop(0, pieces, gate_a, 0)

        @pl.when((k_b >= 0) & (k_b < pieces))
        def _():
            step_b(k_b)

        return 0

    lax.fori_loop(0, last + 1, slot_step, 0)

    def drain(k, _):
        @pl.when(me < n - 1)
        def _():
            remote(out_a.at[k], buf_a.at[k], a_send.at[k], a_recv.at[k], me).wait_send()

        @pl.when(me > 0)
        def _():
            remote(out_b.at[k], buf_b.at[k], b_send.at[k], b_recv.at[k], me).wait_send()

        return 0

    lax.fori_loop(0, pieces, drain, 0)

    def drain_kv(s, _):
        @pl.when(s > me)
        def _():
            for copy in kv_copies(s, s, me, first):
                copy.wait_send()

        @pl.when(s < me)
        def _():
            for copy in kv_copies(s, s, me, both):
                copy.wait_send()

        return 0

    lax.fori_loop(0, n, drain_kv, 0)

    def await_placed(kind, which, src, dst):
        copy = remote(src, dst, o_send.at[kind, which], o_recv.at[kind, which], me)

        @pl.when(block_id(which) // 2 != me)
        def _():
            copy.wait_send()

        copy.wait_recv()

    for which in range(2):
        rows = pl.ds(which * half, half)
        await_placed(pieces, which, ctx_stage.at[rows], ctx_out.at[rows])
    for g in range(groups):
        gcols = slice(g * group_width, (g + 1) * group_width)
        for which in range(2):
            rows = pl.ds(which * half, half)
            for k in range(g * per_group, (g + 1) * per_group):
                cols = pl.ds(k * piece, piece)
                await_placed(k, which, gated.at[rows, cols], arrived.at[rows, cols])
            value = arrived[rows, gcols].astype(F32)
            power = jnp.mean(value * value, axis=-1, keepdims=True)
            mix_out[rows, gcols] = (value * lax.rsqrt(power + NORM_EPS) * gain_ref[:, gcols]).astype(BF16)


def body(n, query, keys, values, m_x, m_z, m_b, m_c, dt_raw, dt_bias, a_log, d_skip, norm_gain):
    tok, width = m_x.shape
    half = tok // 2
    heads = dt_raw.shape[1]
    anywhere = pl.BlockSpec(memory_space=INPUT_SPACE)
    groups = m_b.shape[1] // MN
    piece = math.gcd(width // groups, PIECE)
    pieces = width // piece
    kv = keys.shape[1]
    dma = pltpu.SemaphoreType.DMA
    vmem = pltpu.VMEM
    state = (pieces, MN, piece)
    spec = pl.BlockSpec(memory_space=pltpu.VMEM)
    return pl.pallas_call(
        functools.partial(kernel, n),
        out_shape=(
            jax.ShapeDtypeStruct(query.shape, BF16),
            jax.ShapeDtypeStruct(m_x.shape, BF16),
        ),
        in_specs=[anywhere] * 12,
        out_specs=(spec, spec),
        scratch_shapes=[
            vmem(query.shape, BF16),
            vmem(m_x.shape, BF16),
            vmem(m_x.shape, BF16),
            vmem(m_b.shape, BF16),
            vmem(m_b.shape, BF16),
            vmem((heads, tok), BF16),
            vmem((1, heads), F32),
            vmem((1, heads), F32),
            vmem((1, heads), F32),
            vmem((1, width), F32),
            vmem((n, tok, kv), BF16),
            vmem((n, tok, kv), BF16),
            vmem((tok, n * tok), F32),
            vmem(query.shape, BF16),
            vmem(m_x.shape, BF16),
            vmem(m_x.shape, BF16),
            vmem((tok, width), F32),
            vmem((tok, width), F32),
            vmem((tok, width), BF16),
            vmem((2 * tok + 8, heads), F32),
            vmem((heads, tok), F32),
            vmem((groups, tok, tok), F32),
            vmem(state, BF16),
            vmem(state, BF16),
            vmem(state, BF16),
            vmem(state, BF16),
            vmem(state, F32),
            vmem(state, F32),
            vmem((pieces, 8, piece), F32),
            vmem((pieces, 8, piece), F32),
            dma((n,)),
            dma((n,)),
            dma((n,)),
            dma((n,)),
            dma((pieces,)),
            dma((pieces,)),
            dma((pieces,)),
            dma((pieces,)),
            dma((pieces + 1, 2)),
            dma((pieces + 1, 2)),
            dma((12,)),
        ],
        compiler_params=pltpu.CompilerParams(
            collective_id=0, has_side_effects=True, vmem_limit_bytes=67043328
        ),
    )(
        query, keys, values, m_x, m_z, m_b, m_c, dt_raw.T,
        dt_bias.reshape(1, -1), a_log.reshape(1, -1), d_skip.reshape(1, -1), norm_gain.reshape(1, -1),
    )


def solution(mesh):
    rows = P(("grp", "ctx"), "hd")
    in_specs = (rows,) * 8 + (P("hd"),) * 4
    return jax.shard_map(
        functools.partial(body, mesh.shape["ctx"]),
        mesh=mesh, in_specs=in_specs, out_specs=(rows, rows), check_vma=False,
    )
```

profile of v0, /device:TPU:26, one launch (start us, length us, event | category | flops | bytes accessed | tf_op | source)
XLA Modules:
  0.0 60.4 jit_solution(9378831221821373060)
XLA Ops:
  0.6 57.2 %shard_map.131 = (bf16[128,1024]{1,0:T(8,128)(2,1)}, bf16[128,2048]{1,0:T(8,128)(2,1)}) custom-call(bf16[128,1024]{1,0:T(8,128)(2,1)} %q_in.1, bf16[128,256]{1,0:T(8,128)(2,1)} %k_ref.1, bf16[128,256]{1,0:T(8,128)(2,1)} %v_ref.1, bf16[128,2048]{1,0:T(8,128)(2,1)} %x_in.1, bf16[128,2048]{1,0:T(8,128)(2,1)} %z_in.1, bf16[128,256]{1,0:T(8,128)(2,1)} %b_in.1, ...), custom_call_target="tpu_custom_call" | custom-call | tf_op jit(solution)/shard_map/pallas_call | solution.py:399
  57.9 0.0 copy-start
  57.9 1.7 %copy.16 = bf16[128,1024]{1,0:T(8,128)(2,1)} copy(bf16[128,1024]{1,0:T(8,128)(2,1)} %get-tuple-element.4) | data formatting | bytes 524288
  59.6 0.0 copy-done
  59.6 0.8 %copy.17 = bf16[128,2048]{1,0:T(8,128)(2,1)} copy(bf16[128,2048]{1,0:T(8,128)(2,1)S(1)} %copy-done) | data formatting | bytes 1048576
Async XLA Ops:
  57.9 1.7 %copy-start = (bf16[128,2048]{1,0:T(8,128)(2,1)S(1)}, bf16[128,2048]{1,0:T(8,128)(2,1)}, u32[]{:S(2)}) copy-start(bf16[128,2048]{1,0:T(8,128)(2,1)} %get-tuple-element.5) | copy-start | bytes 1572868
where the time goes:
time: 61.5 us; the launch traced here: 60.4 us
  Pallas kernels  57.2 us (93%)
  local copies, waits for them, and re-layouts  2.52 us (4%)
  between operations  0.65 us (1%)
    pallas_call x1, Pallas kernels, body(): pl.pallas_call(functools.partial(kernel, n), out_shape=(jax.ShapeDtypeStr...  57.2 us
    unnamed x4, local copies, waits for them, and re-layouts  2.52 us

commit v1 on v0

v1 whole, which is shorter than its diff:
```python
import functools
import math

import jax
import jax.numpy as jnp
from jax import lax
from jax.experimental import pallas as pl
from jax.experimental.pallas import tpu as pltpu
from jax.sharding import PartitionSpec as P

HEAD_SIZE = 128
MP = 64
MN = 128
NORM_EPS = 1e-05
MASKED = -1e30
HIGHEST = lax.Precision.HIGHEST
F32 = jnp.float32
BF16 = jnp.bfloat16
INPUT_SPACE = pltpu.HBM
HOP_SLOTS = 2
PIECE = 256


def dot(a, b, ca=1, cb=0, precision=None):
    return lax.dot_general(
        a, b, (((ca,), (cb,)), ((), ())), preferred_element_type=F32, precision=precision
    )


def kernel(
    n, q_in, k_in, v_in, x_in, z_in, b_in, c_in, dt_in, bias_in, alog_in, skip_in,
    gain_in, ctx_out, mix_out,
    q_ref, x_ref, z_ref, b_ref, c_ref, dt_ref, bias_ref, alog_ref, skip_ref, gain_ref,
    kv_all, bias_scr, ctx_stage, arrived, gated, base_scr, er_scr, xdt_scr, hs, runt, gmask,
    buf_a, buf_b, out_a, out_b, sloc_a, sloc_b, tot_a, tot_b, log_in, log_out, wide_t,
    kv_plus, kv_minus, kv_recv, a_send, a_recv, b_send, b_recv, o_send, o_recv, c_send, c_recv,
    log_send, log_recv, load_sem,
):
    me = lax.axis_index("ctx")
    tok = q_ref.shape[0]
    half = tok // 2
    heads = dt_ref.shape[0]
    width = x_ref.shape[1]
    groups = b_ref.shape[1] // MN
    group_width = width // groups
    pieces, _, piece = buf_a.shape
    per_piece = piece // MP
    per_group = group_width // piece
    q_heads = q_ref.shape[1] // HEAD_SIZE
    kv = kv_all.shape[2] // 2
    repeat = q_ref.shape[1] // kv
    mesh_id = pl.DeviceIdType.MESH
    has_left = me > 0
    has_right = me < n - 1

    loads = [
        pltpu.make_async_copy(src, dst, load_sem.at[i])
        for i, (src, dst) in enumerate(
            (
                (dt_in, dt_ref), (bias_in, bias_ref), (alog_in, alog_ref), (skip_in, skip_ref),
                (k_in, kv_all.at[me, :, pl.ds(0, kv)]), (v_in, kv_all.at[me, :, pl.ds(kv, kv)]),
                (b_in, b_ref), (c_in, c_ref), (x_in, x_ref), (z_in, z_ref), (q_in, q_ref),
                (gain_in, gain_ref),
            )
        )
    ]
    for load in loads:
        load.start()

    barrier = pltpu.get_barrier_semaphore()

    def greet(peer):
        pl.semaphore_signal(barrier, inc=1, device_id={"ctx": peer}, device_id_type=mesh_id)

    @pl.when(has_left)
    def _():
        greet(me - 1)

    @pl.when(has_right)
    def _():
        greet(me + 1)

    def remote(src, dst, send, recv, peer):
        return pltpu.make_async_remote_copy(
            src_ref=src, dst_ref=dst, send_sem=send, recv_sem=recv,
            device_id={"ctx": peer}, device_id_type=mesh_id,
        )

    first = pl.ds(0, half)

    def kv_right(s):
        part = kv_all.at[s, first]
        return remote(part, part, kv_plus.at[s], kv_recv.at[s], jnp.minimum(me + 1, n - 1))

    def kv_left(s):
        part = kv_all.at[s]
        return remote(part, part, kv_minus.at[s], kv_recv.at[s], jnp.maximum(me - 1, 0))

    def log_copy():
        return remote(log_out, log_in, log_send, log_recv, jnp.maximum(me - 1, 0))

    row = lax.broadcasted_iota(jnp.int32, (tok, tok), 0)
    col = lax.broadcasted_iota(jnp.int32, (tok, tok), 1)
    for load in loads[:4]:
        load.wait()
    raw = dot((row == col).astype(BF16), dt_ref[...], 1, 1) + bias_ref[...]
    steps = jnp.maximum(raw, 0.0) + jnp.log1p(jnp.exp(-jnp.abs(raw)))
    decay = -steps * jnp.exp(alog_ref[...])
    lower = (col <= row) & ((row < half) == (col < half))
    tri = lower.astype(F32)
    hs[0:tok, :] = dot(tri, decay, precision=HIGHEST)
    hs[tok : 2 * tok, :] = steps
    hs[2 * tok :, :] = jnp.broadcast_to(skip_ref[...], (8, heads))
    runt[...] = dot(decay, tri, 0, 1, precision=HIGHEST)
    own_log = jnp.broadcast_to(hs[half - 1 : half, :] + hs[tok - 1 : tok, :], (8, heads))

    for load in loads[4:6]:
        load.wait()

    pl.semaphore_wait(barrier, has_left.astype(jnp.int32) + has_right.astype(jnp.int32))

    @pl.when(jnp.logical_not(has_right))
    def _():
        log_out[...] = own_log
        log_copy().start()
        kv_left(me).start()

    @pl.when(has_right)
    def _():
        kv_right(me).start()

    @pl.when(has_right & has_left)
    def _():
        kv_left(me).start()

    for load in loads[6:8]:
        load.wait()
    for g in range(groups):
        cols = slice(g * MN, (g + 1) * MN)
        gmask[g] = jnp.where(lower, dot(c_ref[:, cols], b_ref[:, cols], 1, 1), 0.0)

    @pl.when(me == 0)
    def _():
        buf_a[...] = jnp.zeros_like(buf_a)

    @pl.when(me == n - 1)
    def _():
        buf_b[...] = jnp.zeros_like(buf_b)
        wide_t[...] = jnp.ones_like(wide_t)

    lane_head = lax.broadcasted_iota(jnp.int32, (heads, piece), 1) // MP
    head_row = lax.broadcasted_iota(jnp.int32, (heads, piece), 0)
    wide_head = lax.broadcasted_iota(jnp.int32, (heads, per_piece * tok), 1) // tok
    wide_row = lax.broadcasted_iota(jnp.int32, (heads, per_piece * tok), 0)
    left = lax.broadcasted_iota(jnp.int32, (tok, 2 * MP), 1) < MP

    def block_id(which):
        return me if which == 0 else 2 * n - 1 - me

    def put(value, stage, final, rows, cols, send, recv, which):
        owner = block_id(which) // 2
        slot = lax.rem(block_id(which), 2)
        target = pl.ds(pl.multiple_of(slot * half, half), half)

        @pl.when(owner == me)
        def _():
            final[target, cols] = value

        @pl.when(owner != me)
        def _():
            stage[rows, cols] = value
            remote(
                stage.at[rows, cols], final.at[target, cols], send.at[which], recv.at[slot], owner
            ).start()

    def silu(value):
        return value / (1.0 + jnp.exp(-value))

    def prepare(k):
        cols = pl.ds(pl.multiple_of(k * piece, piece), piece)
        gcols = pl.ds(pl.multiple_of((k // per_group) * MN, MN), MN)
        pick = (head_row == k * per_piece + lane_head).astype(F32)
        spread = dot(hs[...], pick, precision=HIGHEST)
        run, step, skip = spread[0:tok], spread[tok : 2 * tok], spread[2 * tok : 2 * tok + 1]
        xs = x_ref[:, cols].astype(F32)
        xdt = xs * step
        last_a, last_b = run[half - 1 : half], run[tok - 1 : tok]
        b_rows = b_ref[:, gcols]
        sloc_a[k] = dot(b_rows[0:half], (xdt[0:half] * jnp.exp(last_a - run[0:half])).astype(BF16), 0, 0)
        sloc_b[k] = dot(b_rows[half:], (xdt[half:] * jnp.exp(last_b - run[half:])).astype(BF16), 0, 0)
        tot_a[k] = jnp.broadcast_to(jnp.exp(last_a), (8, piece))
        tot_b[k] = jnp.broadcast_to(jnp.exp(last_b), (8, piece))
        er_scr[:, cols] = jnp.exp(run)
        xdt_scr[:, cols] = xdt.astype(BF16)
        base_scr[:, cols] = skip * xs

    def within_blocks(k):
        cols = pl.ds(pl.multiple_of(k * piece, piece), piece)
        wide = dot(hs[0:tok, :], (wide_row == k * per_piece + wide_head).astype(F32), precision=HIGHEST)
        gm = gmask[k // per_group]
        inner = []
        for pair in range(per_piece // 2):
            weights = []
            for which in range(2):
                h = 2 * pair + which
                gap = wide[:, h * tok : (h + 1) * tok] - runt[pl.ds(k * per_piece + h, 1), :]
                weights.append((jnp.exp(jnp.minimum(gap, 0.0)) * gm).astype(BF16))
            at = pl.ds(pl.multiple_of(k * piece + pair * 2 * MP, 2 * MP), 2 * MP)
            part = xdt_scr[:, at]
            none = jnp.zeros_like(part)
            stacked = jnp.concatenate([jnp.where(left, part, none), jnp.where(left, none, part)], axis=0)
            inner.append(dot(jnp.concatenate(weights, axis=1), stacked))
        base_scr[:, cols] = base_scr[:, cols] + jnp.concatenate(inner, axis=1)

    def a_copy(k):
        return remote(out_a.at[k], buf_a.at[k], a_send.at[k], a_recv.at[k], jnp.minimum(me + 1, n - 1))

    def b_copy(k):
        return remote(out_b.at[k], buf_b.at[k], b_send.at[k], b_recv.at[k], jnp.maximum(me - 1, 0))

    def step_a(k):
        @pl.when(has_left)
        def _():
            a_copy(k).wait_recv()

        @pl.when(has_right)
        def _():
            out_a[k] = (buf_a[k].astype(F32) * tot_a[k][0:1] + sloc_a[k]).astype(BF16)
            a_copy(k).start()

    def step_b(k):
        cols = pl.ds(pl.multiple_of(k * piece, piece), piece)

        @pl.when(has_right)
        def _():
            b_copy(k).wait_recv()

        @pl.when(has_left)
        def _():
            mine = sloc_a[k] * wide_t[0:1, cols] + buf_b[k].astype(F32)
            out_b[k] = (mine * tot_b[k][0:1] + sloc_b[k]).astype(BF16)
            b_copy(k).start()

    def gate(k, which, state):
        cols = pl.ds(pl.multiple_of(k * piece, piece), piece)
        gcols = pl.ds(pl.multiple_of((k // per_group) * MN, MN), MN)
        rows = slice(which * half, (which + 1) * half)
        carried = dot(c_ref[rows, gcols], state) * er_scr[rows, cols]
        z = z_ref[rows, cols].astype(F32)
        value = ((base_scr[rows, cols] + carried) * silu(z)).astype(BF16)
        put(value, gated, arrived, pl.ds(which * half, half), cols, o_send.at[k], o_recv.at[k], which)

    def gate_a(k):
        gate(k, 0, buf_a[k])

    def gate_b(k):
        cols = pl.ds(pl.multiple_of(k * piece, piece), piece)
        after = buf_a[k].astype(F32) * tot_a[k][0:1] + sloc_a[k]
        entering = after * wide_t[0:1, cols] + buf_b[k].astype(F32)
        gate(k, 1, entering.astype(BF16))

    def take_log():
        @pl.when(has_right)
        def _():
            log_copy().wait_recv()
            later = log_in[...]
            at_head = lax.broadcasted_iota(jnp.int32, (heads, width), 1) // MP
            pick = (lax.broadcasted_iota(jnp.int32, (heads, width), 0) == at_head).astype(F32)

            @pl.when(has_left)
            def _():
                log_out[...] = later + own_log
                log_copy().start()

            wide_t[...] = jnp.exp(dot(later, pick, precision=HIGHEST))

    def relay(h):
        @pl.when(me - h >= 0)
        def _():
            kv_right(jnp.maximum(me - h, 0)).wait_recv()

            @pl.when(has_right)
            def _():
                kv_right(jnp.maximum(me - h, 0)).start()

        @pl.when(me + h < n)
        def _():
            kv_left(jnp.minimum(me + h, n - 1)).wait_recv()

            @pl.when(has_left)
            def _():
                kv_left(jnp.minimum(me + h, n - 1)).start()

    def attention_mask():
        def clear(s, _):
            @pl.when(s < me)
            def _():
                kv_all[s, half:, :] = jnp.zeros((half, 2 * kv), BF16)

            return 0

        lax.fori_loop(0, n, clear, 0)
        key = lax.broadcasted_iota(jnp.int32, (tok, n * tok), 1)
        source = key // tok
        within = key - source * tok
        key_pos = jnp.where(
            within < half, source * half + within, (2 * n - 2 - source) * half + within
        )
        query = lax.broadcasted_iota(jnp.int32, (tok, n * tok), 0)
        query_pos = jnp.where(query < half, me * half + query, (2 * n - 2 - me) * half + query)
        bias_scr[...] = jnp.where(key_pos <= query_pos, 0.0, MASKED)

    scale = 1.0 / math.sqrt(HEAD_SIZE)

    def one_head(h):
        hcols = pl.ds(pl.multiple_of(h * HEAD_SIZE, HEAD_SIZE), HEAD_SIZE)
        kcols = pl.ds(pl.multiple_of((h // repeat) * HEAD_SIZE, HEAD_SIZE), HEAD_SIZE)
        vcols = pl.ds(pl.multiple_of(kv + (h // repeat) * HEAD_SIZE, HEAD_SIZE), HEAD_SIZE)
        keys = kv_all[:, :, kcols].reshape(n * tok, HEAD_SIZE)
        values = kv_all[:, :, vcols].reshape(n * tok, HEAD_SIZE)
        scores = dot(q_ref[:, hcols], keys, 1, 1) * scale + bias_scr[...]
        expo = jnp.exp(scores - jnp.max(scores, axis=-1, keepdims=True))
        total = jnp.sum(expo, axis=-1, keepdims=True)
        value = (dot(expo.astype(BF16), values) / total).astype(BF16)
        for which in range(2):
            rows = slice(which * half, (which + 1) * half)
            put(value[rows], ctx_stage, ctx_out, pl.ds(which * half, half), hcols, c_send.at[h], c_recv.at[h], which)

    for load in loads[8:11]:
        load.wait()
    attention_mask()
    lag_a = me * HOP_SLOTS
    lag_b = (n - 1 - me) * HOP_SLOTS
    lag = jnp.maximum(lag_a, lag_b)
    attend = (n - 1) * HOP_SLOTS
    last = (n - 1) * HOP_SLOTS + max(pieces, q_heads)

    def slot_step(t, _):
        @pl.when(t < pieces)
        def _():
            prepare(t)

        @pl.when((t >= lag_a) & (t < lag_a + pieces))
        def _():
            step_a(t - lag_a)

        @pl.when(t == lag_b)
        def _():
            take_log()

        @pl.when((t >= lag_b) & (t < lag_b + pieces))
        def _():
            step_b(t - lag_b)

        @pl.when((t > 0) & (lax.rem(t, HOP_SLOTS) == 0) & (t <= (n - 1) * HOP_SLOTS))
        def _():
            relay(t // HOP_SLOTS)

        @pl.when(t < pieces)
        def _():
            within_blocks(t)

        @pl.when((t >= lag_a) & (t < lag_a + pieces))
        def _():
            gate_a(t - lag_a)

        @pl.when((t >= lag) & (t < lag + pieces))
        def _():
            gate_b(t - lag)

        @pl.when((t >= attend) & (t < attend + q_heads))
        def _():
            one_head(t - attend)

        return 0

    lax.fori_loop(0, last, slot_step, 0)

    def drain(k, _):
        @pl.when(has_right)
        def _():
            a_copy(k).wait_send()

        @pl.when(has_left)
        def _():
            b_copy(k).wait_send()

        return 0

    lax.fori_loop(0, pieces, drain, 0)

    @pl.when(has_left)
    def _():
        log_copy().wait_send()

    def drain_kv(s, _):
        @pl.when((s <= me) & has_right)
        def _():
            kv_right(s).wait_send()

        @pl.when((s >= me) & has_left)
        def _():
            kv_left(s).wait_send()

        return 0

    lax.fori_loop(0, n, drain_kv, 0)

    def settle(stage, final, cols, send, recv):
        for which in range(2):
            rows = pl.ds(which * half, half)
            copy = remote(stage.at[rows, cols], final.at[rows, cols], send.at[which], recv.at[which], me)

            @pl.when(block_id(which) // 2 != me)
            def _():
                copy.wait_send()

        for slot in range(2):
            source = jnp.where(2 * me + slot < n, 2 * me + slot, 2 * n - 1 - 2 * me - slot)
            rows = pl.ds(slot * half, half)
            copy = remote(stage.at[rows, cols], final.at[rows, cols], send.at[slot], recv.at[slot], me)

            @pl.when(source != me)
            def _():
                copy.wait_recv()

    for h in range(q_heads):
        settle(ctx_stage, ctx_out, pl.ds(h * HEAD_SIZE, HEAD_SIZE), c_send.at[h], c_recv.at[h])
    loads[11].wait()
    for g in range(groups):
        gcols = slice(g * group_width, (g + 1) * group_width)
        for k in range(g * per_group, (g + 1) * per_group):
            settle(gated, arrived, pl.ds(k * piece, piece), o_send.at[k], o_recv.at[k])
        for which in range(2):
            rows = pl.ds(which * half, half)
            value = arrived[rows, gcols].astype(F32)
            power = jnp.mean(value * value, axis=-1, keepdims=True)
            mix_out[rows, gcols] = (value * lax.rsqrt(power + NORM_EPS) * gain_ref[:, gcols]).astype(BF16)


def body(n, query, keys, values, m_x, m_z, m_b, m_c, dt_raw, dt_bias, a_log, d_skip, norm_gain):
    tok, width = m_x.shape
    half = tok // 2
    heads = dt_raw.shape[1]
    anywhere = pl.BlockSpec(memory_space=INPUT_SPACE)
    groups = m_b.shape[1] // MN
    piece = math.gcd(width // groups, PIECE)
    pieces = width // piece
    kv = keys.shape[1]
    q_heads = query.shape[1] // HEAD_SIZE
    dma = pltpu.SemaphoreType.DMA
    vmem = pltpu.VMEM
    state = (pieces, MN, piece)
    spec = pl.BlockSpec(memory_space=pltpu.VMEM)
    return pl.pallas_call(
        functools.partial(kernel, n),
        out_shape=(
            jax.ShapeDtypeStruct(query.shape, BF16),
            jax.ShapeDtypeStruct(m_x.shape, BF16),
        ),
        in_specs=[anywhere] * 12,
        out_specs=(spec, spec),
        scratch_shapes=[
            vmem(query.shape, BF16),
            vmem(m_x.shape, BF16),
            vmem(m_x.shape, BF16),
            vmem(m_b.shape, BF16),
            vmem(m_b.shape, BF16),
            vmem((heads, tok), BF16),
            vmem((1, heads), F32),
            vmem((1, heads), F32),
            vmem((1, heads), F32),
            vmem((1, width), F32),
            vmem((n, tok, 2 * kv), BF16),
            vmem((tok, n * tok), F32),
            vmem(query.shape, BF16),
            vmem(m_x.shape, BF16),
            vmem(m_x.shape, BF16),
            vmem((tok, width), F32),
            vmem((tok, width), F32),
            vmem((tok, width), BF16),
            vmem((2 * tok + 8, heads), F32),
            vmem((heads, tok), F32),
            vmem((groups, tok, tok), F32),
            vmem(state, BF16),
            vmem(state, BF16),
            vmem(state, BF16),
            vmem(state, BF16),
            vmem(state, F32),
            vmem(state, F32),
            vmem((pieces, 8, piece), F32),
            vmem((pieces, 8, piece), F32),
            vmem((8, heads), F32),
            vmem((8, heads), F32),
            vmem((8, width), F32),
            dma((n,)),
            dma((n,)),
            dma((n,)),
            dma((pieces,)),
            dma((pieces,)),
            dma((pieces,)),
            dma((pieces,)),
            dma((pieces, 2)),
            dma((pieces, 2)),
            dma((q_heads, 2)),
            dma((q_heads, 2)),
            dma(()),
            dma(()),
            dma((12,)),
        ],
        compiler_params=pltpu.CompilerParams(
            collective_id=0, has_side_effects=True, vmem_limit_bytes=67043328
        ),
    )(
        query, keys, values, m_x, m_z, m_b, m_c, dt_raw.T,
        dt_bias.reshape(1, -1), a_log.reshape(1, -1), d_skip.reshape(1, -1), norm_gain.reshape(1, -1),
    )


def solution(mesh):
    rows = P(("grp", "ctx"), "hd")
    in_specs = (rows,) * 8 + (P("hd"),) * 4
    return jax.shard_map(
        functools.partial(body, mesh.shape["ctx"]),
        mesh=mesh, in_specs=in_specs, out_specs=(rows, rows), check_vma=False,
    )
```

time: 61.5 us -> 51.6 us (0.84)
  the two profiles are of different devices: /device:TPU:26 before, /device:TPU:8 now
where the time goes in v1:
time: 51.6 us; the launch traced here: 51.4 us
  Pallas kernels  48.2 us (93%)
  local copies, waits for them, and re-layouts  2.52 us (5%)
  between operations  0.65 us (1%)
    pallas_call x1, Pallas kernels, body(): pl.pallas_call(functools.partial(kernel, n), out_shape=(jax.ShapeDtypeStr...  48.2 us
    unnamed x4, local copies, waits for them, and re-layouts  2.52 us

profile of v1, /device:TPU:8, one launch (start us, length us, event | category | flops | bytes accessed | tf_op | source)
XLA Modules:
  0.0 51.4 jit_solution(13470839430235801406)
XLA Ops:
  0.6 48.2 %shard_map.131 = (bf16[128,1024]{1,0:T(8,128)(2,1)}, bf16[128,2048]{1,0:T(8,128)(2,1)}) custom-call(bf16[128,1024]{1,0:T(8,128)(2,1)} %q_in.1, bf16[128,256]{1,0:T(8,128)(2,1)} %k_in.1, bf16[128,256]{1,0:T(8,128)(2,1)} %v_in.1, bf16[128,2048]{1,0:T(8,128)(2,1)} %x_in.1, bf16[128,2048]{1,0:T(8,128)(2,1)} %z_in.1, bf16[128,256]{1,0:T(8,128)(2,1)} %b_in.1, ...), custom_call_target="tpu_custom_call" | custom-call | tf_op jit(solution)/shard_map/pallas_call | solution.py:455
  48.8 0.0 copy-start
  48.8 1.7 %copy.16 = bf16[128,1024]{1,0:T(8,128)(2,1)} copy(bf16[128,1024]{1,0:T(8,128)(2,1)} %get-tuple-element.4) | data formatting | bytes 524288
  50.6 0.0 copy-done
  50.6 0.8 %copy.17 = bf16[128,2048]{1,0:T(8,128)(2,1)} copy(bf16[128,2048]{1,0:T(8,128)(2,1)S(1)} %copy-done) | data formatting | bytes 1048576
Async XLA Ops:
  48.8 1.7 %copy-start = (bf16[128,2048]{1,0:T(8,128)(2,1)S(1)}, bf16[128,2048]{1,0:T(8,128)(2,1)}, u32[]{:S(2)}) copy-start(bf16[128,2048]{1,0:T(8,128)(2,1)} %get-tuple-element.5) | copy-start | bytes 1572868

commit v2 on v1

v2 whole, which is shorter than its diff:
```python
import functools
import math

import jax
import jax.numpy as jnp
from jax import lax
from jax.experimental import pallas as pl
from jax.experimental.pallas import tpu as pltpu
from jax.sharding import PartitionSpec as P

HEAD_SIZE = 128
MP = 64
MN = 128
NORM_EPS = 1e-05
MASKED = -1e30
HIGHEST = lax.Precision.HIGHEST
F32 = jnp.float32
BF16 = jnp.bfloat16
INPUT_SPACE = pltpu.HBM
PIECE = 256


def dot(a, b, ca=1, cb=0, precision=None):
    return lax.dot_general(
        a, b, (((ca,), (cb,)), ((), ())), preferred_element_type=F32, precision=precision
    )


def split(value):
    high = value.astype(BF16)
    rest = value - high.astype(F32)
    mid = rest.astype(BF16)
    return high, mid, (rest - mid.astype(F32)).astype(BF16)


def kernel(
    n, wide_hd, q_in, k_in, v_in, x_in, z_in, b_in, c_in, dt_in, bias_in, alog_in, skip_in,
    gain_in, ctx_out, mix_out,
    q_ref, x_ref, z_ref, b_ref, c_ref, dt_ref, bias_ref, alog_ref, skip_ref, gain_ref,
    kv_all, bias_scr, ctx_stage, arrived, gated, base_scr, er_scr, xdt_scr, hs, run_split, gmask,
    buf_a, buf_b, out_a, out_b, sloc_a, sloc_b, tot_a, tot_b, log_in, log_out, wide_t,
    kv_plus, kv_minus, kv_recv, a_send, a_recv, b_send, b_recv, o_send, o_recv, c_send, c_recv,
    log_send, log_recv, plus_sem, minus_sem, pair_plus, pair_minus, load_sem,
):
    me = lax.axis_index("ctx")
    tok = q_ref.shape[0]
    half = tok // 2
    heads = dt_ref.shape[0]
    width = x_ref.shape[1]
    groups = b_ref.shape[1] // MN
    group_width = width // groups
    pieces, _, piece = buf_a.shape
    per_piece = piece // MP
    per_group = group_width // piece
    q_heads = q_ref.shape[1] // HEAD_SIZE
    kv = kv_all.shape[2] // 2
    repeat = q_ref.shape[1] // kv
    mesh_id = pl.DeviceIdType.MESH
    core = lax.axis_index("hd")
    paired = wide_hd % 2 == 0
    partner = core + 1 - 2 * lax.rem(core, 2)
    has_left = me > 0
    has_right = me < n - 1

    loads = [
        pltpu.make_async_copy(src, dst, load_sem.at[i])
        for i, (src, dst) in enumerate(
            (
                (dt_in, dt_ref), (bias_in, bias_ref), (alog_in, alog_ref), (skip_in, skip_ref),
                (k_in, kv_all.at[me, :, pl.ds(0, kv)]), (v_in, kv_all.at[me, :, pl.ds(kv, kv)]),
                (b_in, b_ref), (c_in, c_ref), (x_in, x_ref), (z_in, z_ref), (q_in, q_ref),
                (gain_in, gain_ref),
            )
        )
    ]
    for load in loads:
        load.start()

    barrier = pltpu.get_barrier_semaphore()

    def greet(peer):
        pl.semaphore_signal(barrier, inc=1, device_id={"ctx": peer}, device_id_type=mesh_id)

    @pl.when(has_left)
    def _():
        greet(me - 1)

    @pl.when(has_right)
    def _():
        greet(me + 1)

    if paired:
        pl.semaphore_signal(barrier, inc=1, device_id={"hd": partner}, device_id_type=mesh_id)

    def remote(src, dst, send, recv, peer):
        return pltpu.make_async_remote_copy(
            src_ref=src, dst_ref=dst, send_sem=send, recv_sem=recv,
            device_id={"ctx": peer}, device_id_type=mesh_id,
        )

    first = pl.ds(0, half)

    def kv_right(s):
        part = kv_all.at[s, first]
        return remote(part, part, kv_plus.at[s], kv_recv.at[s, 0], jnp.minimum(me + 1, n - 1))

    def kv_left(s):
        copies = []
        for i in range(2):
            part = kv_all.at[s, pl.ds(i * half, half)]
            copies.append(
                remote(part, part, kv_minus.at[s, i], kv_recv.at[s, i], jnp.maximum(me - 1, 0))
            )
        return copies

    def log_copy():
        return remote(log_out, log_in, log_send, log_recv, jnp.maximum(me - 1, 0))

    row = lax.broadcasted_iota(jnp.int32, (tok, tok), 0)
    col = lax.broadcasted_iota(jnp.int32, (tok, tok), 1)
    for load in loads[:4]:
        load.wait()
    raw = dot((row == col).astype(BF16), dt_ref[...], 1, 1) + bias_ref[...]
    steps = jnp.maximum(raw, 0.0) + jnp.log1p(jnp.exp(-jnp.abs(raw)))
    decay = -steps * jnp.exp(alog_ref[...])
    lower = (col <= row) & ((row < half) == (col < half))
    tri = lower.astype(BF16)
    high, mid, low = split(decay)
    run = dot(tri, high) + dot(tri, mid) + dot(tri, low)
    ends = jnp.where(
        lax.broadcasted_iota(jnp.int32, (tok, heads), 0) < half, run[half - 1 : half], run[tok - 1 : tok]
    )

    def keep_split(ref, start, value):
        for i, part in enumerate(split(value)):
            ref[start : start + value.shape[0], i * heads : (i + 1) * heads] = part

    keep_split(run_split, 0, run)
    keep_split(hs, 0, jnp.exp(run))
    keep_split(hs, tok, jnp.exp(ends - run) * steps)
    keep_split(hs, 2 * tok, steps)
    keep_split(hs, 3 * tok, jnp.broadcast_to(skip_ref[...], (16, heads)))
    own_log = jnp.broadcast_to(run[half - 1 : half] + run[tok - 1 : tok], (8, heads))

    for load in loads[4:6]:
        load.wait()

    pl.semaphore_wait(barrier, has_left.astype(jnp.int32) + has_right.astype(jnp.int32) + int(paired))

    @pl.when(jnp.logical_not(has_right))
    def _():
        log_out[...] = own_log
        log_copy().start()

    @pl.when(has_right & has_left)
    def _():
        kv_right(me).start()
        for copy in kv_left(me):
            copy.start()

    for load in loads[6:8]:
        load.wait()
    lanes = per_piece * half
    lane = lax.broadcasted_iota(jnp.int32, (half, lanes), 1)
    source = lane - lane // half * half
    target = lax.broadcasted_iota(jnp.int32, (half, lanes), 0)
    causal = source <= target
    diagonal = source == target
    for g in range(groups):
        cols = slice(g * MN, (g + 1) * MN)
        for which in range(2):
            rows = slice(which * half, (which + 1) * half)
            repeated = jnp.concatenate([b_ref[rows, cols]] * per_piece, axis=0)
            gmask[g, rows, :] = jnp.where(causal, dot(c_ref[rows, cols], repeated, 1, 1), 0.0)

    @pl.when(me == 0)
    def _():
        buf_a[...] = jnp.zeros_like(buf_a)

    @pl.when(me == n - 1)
    def _():
        buf_b[...] = jnp.zeros_like(buf_b)
        wide_t[...] = jnp.ones_like(wide_t)

    split_head = lax.rem(lax.broadcasted_iota(jnp.int32, (3 * heads, piece), 0), heads)
    lane_head = lax.broadcasted_iota(jnp.int32, (3 * heads, piece), 1) // MP
    wide_head = lax.rem(lax.broadcasted_iota(jnp.int32, (3 * heads, lanes), 0), heads)
    wide_lane = lax.broadcasted_iota(jnp.int32, (3 * heads, lanes), 1) // half
    part_head = lax.broadcasted_iota(jnp.int32, (half, piece), 1) // MP

    def block_id(which):
        return me if which == 0 else 2 * n - 1 - me

    def send(stage, final, cols, send_sem, recv_sem, which):
        owner = block_id(which) // 2
        slot = lax.rem(block_id(which), 2)
        rows = pl.ds(which * half, half)
        target = pl.ds(pl.multiple_of(slot * half, half), half)

        @pl.when(owner == me)
        def _():
            final[target, cols] = stage[rows, cols]

        @pl.when(owner != me)
        def _():
            remote(
                stage.at[rows, cols], final.at[target, cols], send_sem.at[which], recv_sem.at[slot], owner
            ).start()

    def silu(value):
        return value / (1.0 + jnp.exp(-value))

    def prepare(k):
        cols = pl.ds(pl.multiple_of(k * piece, piece), piece)
        gcols = pl.ds(pl.multiple_of((k // per_group) * MN, MN), MN)
        spread = dot(hs[...], (split_head == k * per_piece + lane_head).astype(BF16))
        xs = x_ref[:, cols].astype(F32)
        weighted = (xs * spread[tok : 2 * tok]).astype(BF16)
        b_rows = b_ref[:, gcols]
        sloc_a[k] = dot(b_rows[0:half], weighted[0:half], 0, 0)
        sloc_b[k] = dot(b_rows[half:], weighted[half:], 0, 0)
        tot_a[k] = jnp.broadcast_to(spread[half - 1 : half], (8, piece))
        tot_b[k] = jnp.broadcast_to(spread[tok - 1 : tok], (8, piece))
        er_scr[:, cols] = spread[0:tok]
        xdt_scr[:, cols] = (xs * spread[2 * tok : 3 * tok]).astype(BF16)
        base_scr[:, cols] = spread[3 * tok : 3 * tok + 1] * xs

    def within_blocks(k):
        cols = pl.ds(pl.multiple_of(k * piece, piece), piece)
        wide = dot(run_split[...], (wide_head == k * per_piece + wide_lane).astype(BF16))
        for which in range(2):
            rows = slice(which * half, (which + 1) * half)
            mine = wide[rows]
            gap = mine - jnp.sum(jnp.where(diagonal, mine, 0.0), axis=0, keepdims=True)
            weights = (jnp.exp(jnp.minimum(gap, 0.0)) * gmask[k // per_group, rows, :]).astype(BF16)
            part = xdt_scr[rows, cols]
            none = jnp.zeros_like(part)
            stacked = jnp.concatenate(
                [jnp.where(part_head == h, part, none) for h in range(per_piece)], axis=0
            )
            base_scr[rows, cols] = base_scr[rows, cols] + dot(weights, stacked)

    def a_copy(k):
        return remote(out_a.at[k], buf_a.at[k], a_send.at[k], a_recv.at[k], jnp.minimum(me + 1, n - 1))

    def b_copy(k):
        return remote(out_b.at[k], buf_b.at[k], b_send.at[k], b_recv.at[k], jnp.maximum(me - 1, 0))

    def step_a(k):
        @pl.when(has_left)
        def _():
            a_copy(k).wait_recv()

        @pl.when(has_right)
        def _():
            out_a[k] = (buf_a[k].astype(F32) * tot_a[k][0:1] + sloc_a[k]).astype(BF16)
            a_copy(k).start()

    def step_b(k):
        cols = pl.ds(pl.multiple_of(k * piece, piece), piece)

        @pl.when(has_right)
        def _():
            b_copy(k).wait_recv()

        @pl.when(has_left)
        def _():
            mine = sloc_a[k] * wide_t[0:1, cols] + buf_b[k].astype(F32)
            out_b[k] = (mine * tot_b[k][0:1] + sloc_b[k]).astype(BF16)
            b_copy(k).start()

    def gate(k, which, state):
        cols = pl.ds(pl.multiple_of(k * piece, piece), piece)
        gcols = pl.ds(pl.multiple_of((k // per_group) * MN, MN), MN)
        rows = slice(which * half, (which + 1) * half)
        carried = dot(c_ref[rows, gcols], state) * er_scr[rows, cols]
        z = z_ref[rows, cols].astype(F32)
        value = ((base_scr[rows, cols] + carried) * silu(z)).astype(BF16)
        gated[rows, cols] = value

    def send_gated(k):
        cols = pl.ds(pl.multiple_of(k * piece, piece), piece)
        for which in range(2):
            send(gated, arrived, cols, o_send.at[k], o_recv.at[k], which)

    def gate_a(k):
        gate(k, 0, buf_a[k])

    def gate_b(k):
        cols = pl.ds(pl.multiple_of(k * piece, piece), piece)
        after = buf_a[k].astype(F32) * tot_a[k][0:1] + sloc_a[k]
        entering = after * wide_t[0:1, cols] + buf_b[k].astype(F32)
        gate(k, 1, entering.astype(BF16))

    def take_log():
        @pl.when(has_right)
        def _():
            log_copy().wait_recv()
            later = log_in[...]
            @pl.when(has_left)
            def _():
                log_out[...] = later + own_log
                log_copy().start()

            shape = (heads, width)
            pick = lax.broadcasted_iota(jnp.int32, shape, 0) == lax.broadcasted_iota(jnp.int32, shape, 1) // MP
            high, mid, low = split(jnp.exp(later))
            pick = pick.astype(BF16)
            wide_t[...] = dot(high, pick) + dot(mid, pick) + dot(low, pick)

    def relay_right(h):
        source = jnp.maximum(me - h, 0)

        @pl.when(source != me)
        def _():
            kv_right(source).wait_recv()

        @pl.when(has_right)
        def _():
            kv_right(source).start()

    def relay_left(h):
        source = jnp.minimum(me + h, n - 1)
        for copy in kv_left(source):
            @pl.when(source != me)
            def _(copy=copy):
                copy.wait_recv()

            @pl.when(has_left)
            def _(copy=copy):
                copy.start()

    def attention_mask():
        def clear(s, _):
            @pl.when(s < me)
            def _():
                kv_all[s, half:, :] = jnp.zeros((half, 2 * kv), BF16)

            return 0

        lax.fori_loop(0, n, clear, 0)
        key = lax.broadcasted_iota(jnp.int32, (tok, n * tok), 1)
        source = key // tok
        within = key - source * tok
        key_pos = jnp.where(
            within < half, source * half + within, (2 * n - 2 - source) * half + within
        )
        query = lax.broadcasted_iota(jnp.int32, (tok, n * tok), 0)
        query_pos = jnp.where(query < half, me * half + query, (2 * n - 2 - me) * half + query)
        bias_scr[...] = jnp.where(key_pos <= query_pos, 0.0, MASKED)

    scale = 1.0 / math.sqrt(HEAD_SIZE)

    def one_head(h):
        hcols = pl.ds(pl.multiple_of(h * HEAD_SIZE, HEAD_SIZE), HEAD_SIZE)
        kcols = pl.ds(pl.multiple_of((h // repeat) * HEAD_SIZE, HEAD_SIZE), HEAD_SIZE)
        vcols = pl.ds(pl.multiple_of(kv + (h // repeat) * HEAD_SIZE, HEAD_SIZE), HEAD_SIZE)
        keys = kv_all[:, :, kcols].reshape(n * tok, HEAD_SIZE)
        values = kv_all[:, :, vcols].reshape(n * tok, HEAD_SIZE)
        scores = dot(q_ref[:, hcols], keys, 1, 1) * scale + bias_scr[...]
        expo = jnp.exp(scores - jnp.max(scores, axis=-1, keepdims=True))
        total = jnp.sum(expo, axis=-1, keepdims=True)
        ctx_stage[:, hcols] = (dot(expo.astype(BF16), values) / total).astype(BF16)

    def send_ctx():
        for which in range(2):
            send(ctx_stage, ctx_out, slice(None), c_send, c_recv, which)

    for load in loads[8:11]:
        load.wait()
    attention_mask()
    hops = n - 1 - me
    middle = pieces // 2

    def first_step(k, _):
        prepare(k)

        @pl.when((k == middle) & (me == 0))
        def _():
            relay_right(0)

        @pl.when((k == middle) & (me == n - 1))
        def _():
            relay_left(0)

        @pl.when(me == 0)
        def _():
            step_a(k)

        @pl.when(me == n - 1)
        def _():
            step_b(k)

        return 0

    lax.fori_loop(0, pieces, first_step, 0)

    def base(distance):
        return (9 * jnp.maximum(distance - 1, 0)) // 4

    lag_a = base(me)
    lag_b = base(hops)
    block_b = 2 * n - 1 - me
    hold_plus = block_b // 2 - 1 > me
    hold_minus = me // 2 + 1 < me
    gap = jnp.where(hops > 1, 2, 1)
    attend = 1 + jnp.maximum(
        jnp.where(has_left, lag_a + middle, 0), jnp.where(has_right, lag_b + middle + gap, 0)
    )
    gates = jnp.maximum(lag_a + middle + 1, lag_b + middle + gap + 1)
    gates = gates + jnp.where(2 * me < n, jnp.where(has_left, 2, 1), jnp.where(has_right, 3, 1))
    gates = jnp.maximum(gates, jnp.where(hold_plus, lag_a + pieces + 1, 0))
    gates = jnp.maximum(gates, jnp.where(hold_minus, lag_b + pieces + gap + 1, 0))
    place_ctx = jnp.maximum(attend + q_heads // 2 - 1, gates)
    last = functools.reduce(jnp.maximum, [
        lag_a + pieces + 2, lag_b + pieces + gap + 2, attend + q_heads // 2, place_ctx + 1,
        gates + middle, 3 * n,
    ])

    def passed(pair_sem, sem, peers, wait):
        any_peer = functools.reduce(jnp.logical_or, [ok for _, ok in peers])

        @pl.when(any_peer)
        def _():
            if paired and not wait:
                pl.semaphore_signal(pair_sem, inc=1, device_id={"hd": partner}, device_id_type=mesh_id)
            elif paired:
                pl.semaphore_wait(pair_sem, 1)

        if wait:
            for peer, ok in peers:
                @pl.when(ok)
                def _(peer=peer):
                    pl.semaphore_signal(sem, inc=1, device_id={"ctx": peer}, device_id_type=mesh_id)

    plus_peers = [(p, (p >= 0) & (p < me)) for p in (2 * n - 3 - 2 * me, 2 * n - 4 - 2 * me)]
    minus_peers = [(p, (p > me) & (p < n)) for p in (2 * me - 2, 2 * me - 1)]
    plus_peers = [(p, ok & has_right) for p, ok in plus_peers]
    minus_peers = [(p, ok & has_left) for p, ok in minus_peers]

    def chain_a(t):
        at = t - lag_a

        @pl.when((at == middle) & has_left)
        def _():
            relay_right(me)

        k = jnp.where(at < middle, at, at - 1)

        @pl.when((at >= 0) & (at <= pieces) & (at != middle) & has_left)
        def _():
            step_a(k)

        @pl.when((at == pieces) & has_left)
        def _():
            passed(pair_plus, plus_sem, plus_peers, False)

        @pl.when((at == pieces + 1) & has_left)
        def _():
            passed(pair_plus, plus_sem, plus_peers, True)

    def chain_b(t):
        at = t - lag_b

        @pl.when((at == 0) & has_right)
        def _():
            take_log()

        @pl.when((at == middle + gap) & has_right)
        def _():
            relay_left(hops)

        k = jnp.where(at < middle, at, at - gap - 1)

        @pl.when(((at >= 0) & (at < middle) | (at > middle + gap) & (at <= pieces + gap)) & has_right)
        def _():
            step_b(k)

        @pl.when((at == pieces + gap) & has_right)
        def _():
            passed(pair_minus, minus_sem, minus_peers, False)

        @pl.when((at == pieces + gap + 1) & has_right)
        def _():
            passed(pair_minus, minus_sem, minus_peers, True)

    def slot_step(t, _):
        @pl.when(2 * me >= n)
        def _():
            chain_b(t)

        chain_a(t)

        @pl.when(2 * me < n)
        def _():
            chain_b(t)

        for h in range(1, n - 1):
            @pl.when((t == 2 * h - 2) & (h < me))
            def _(h=h):
                relay_right(h)

            @pl.when((t == 3 * h - 2) & (h < hops))
            def _(h=h):
                relay_left(h)

        @pl.when(t < pieces)
        def _():
            within_blocks(t)

        @pl.when((t >= attend) & (t < attend + q_heads // 2))
        def _():
            one_head(2 * (t - attend))
            one_head(2 * (t - attend) + 1)

        @pl.when((t == gates) & hold_plus)
        def _():
            pl.semaphore_wait(plus_sem, 1)

        @pl.when((t == gates) & hold_minus)
        def _():
            pl.semaphore_wait(minus_sem, 1)

        @pl.when(t == place_ctx)
        def _():
            send_ctx()

        @pl.when((t >= gates) & (t < gates + middle))
        def _():
            for i in range(2):
                gate_a(2 * (t - gates) + i)
                gate_b(2 * (t - gates) + i)
            for i in range(2):
                send_gated(2 * (t - gates) + i)

        return 0

    lax.fori_loop(0, last, slot_step, 0)

    def drain(k, _):
        @pl.when(has_right)
        def _():
            a_copy(k).wait_send()

        @pl.when(has_left)
        def _():
            b_copy(k).wait_send()

        return 0

    lax.fori_loop(0, pieces, drain, 0)

    @pl.when(has_left)
    def _():
        log_copy().wait_send()

    def drain_kv(s, _):
        @pl.when((s <= me) & has_right)
        def _():
            kv_right(s).wait_send()

        @pl.when((s >= me) & has_left)
        def _():
            for copy in kv_left(s):
                copy.wait_send()

        return 0

    lax.fori_loop(0, n, drain_kv, 0)

    def settle(stage, final, cols, send_sem, recv_sem):
        for which in range(2):
            rows = pl.ds(which * half, half)
            copy = remote(stage.at[rows, cols], final.at[rows, cols], send_sem.at[which], recv_sem.at[which], me)

            @pl.when(block_id(which) // 2 != me)
            def _():
                copy.wait_send()

        for slot in range(2):
            source = jnp.where(2 * me + slot < n, 2 * me + slot, 2 * n - 1 - 2 * me - slot)
            rows = pl.ds(slot * half, half)
            copy = remote(stage.at[rows, cols], final.at[rows, cols], send_sem.at[slot], recv_sem.at[slot], me)

            @pl.when(source != me)
            def _():
                copy.wait_recv()

    settle(ctx_stage, ctx_out, slice(None), c_send, c_recv)
    loads[11].wait()
    for g in range(groups):
        gcols = slice(g * group_width, (g + 1) * group_width)
        for k in range(g * per_group, (g + 1) * per_group):
            settle(gated, arrived, pl.ds(k * piece, piece), o_send.at[k], o_recv.at[k])
        for which in range(2):
            rows = pl.ds(which * half, half)
            value = arrived[rows, gcols].astype(F32)
            power = jnp.mean(value * value, axis=-1, keepdims=True)
            mix_out[rows, gcols] = (value * lax.rsqrt(power + NORM_EPS) * gain_ref[:, gcols]).astype(BF16)


def body(n, wide_hd, query, keys, values, m_x, m_z, m_b, m_c, dt_raw, dt_bias, a_log, d_skip, norm_gain):
    tok, width = m_x.shape
    half = tok // 2
    heads = dt_raw.shape[1]
    anywhere = pl.BlockSpec(memory_space=INPUT_SPACE)
    groups = m_b.shape[1] // MN
    piece = math.gcd(width // groups, PIECE)
    pieces = width // piece
    kv = keys.shape[1]
    q_heads = query.shape[1] // HEAD_SIZE
    dma = pltpu.SemaphoreType.DMA
    vmem = pltpu.VMEM
    state = (pieces, MN, piece)
    spec = pl.BlockSpec(memory_space=pltpu.VMEM)
    return pl.pallas_call(
        functools.partial(kernel, n, wide_hd),
        out_shape=(
            jax.ShapeDtypeStruct(query.shape, BF16),
            jax.ShapeDtypeStruct(m_x.shape, BF16),
        ),
        in_specs=[anywhere] * 12,
        out_specs=(spec, spec),
        scratch_shapes=[
            vmem(query.shape, BF16),
            vmem(m_x.shape, BF16),
            vmem(m_x.shape, BF16),
            vmem(m_b.shape, BF16),
            vmem(m_b.shape, BF16),
            vmem((heads, tok), BF16),
            vmem((1, heads), F32),
            vmem((1, heads), F32),
            vmem((1, heads), F32),
            vmem((1, width), F32),
            vmem((n, tok, 2 * kv), BF16),
            vmem((tok, n * tok), F32),
            vmem(query.shape, BF16),
            vmem(m_x.shape, BF16),
            vmem(m_x.shape, BF16),
            vmem((tok, width), F32),
            vmem((tok, width), F32),
            vmem((tok, width), BF16),
            vmem((3 * tok + 16, 3 * heads), BF16),
            vmem((tok, 3 * heads), BF16),
            vmem((groups, tok, piece // MP * (tok // 2)), F32),
            vmem(state, BF16),
            vmem(state, BF16),
            vmem(state, BF16),
            vmem(state, BF16),
            vmem(state, F32),
            vmem(state, F32),
            vmem((pieces, 8, piece), F32),
            vmem((pieces, 8, piece), F32),
            vmem((8, heads), F32),
            vmem((8, heads), F32),
            vmem((8, width), F32),
            dma((n,)),
            dma((n, 2)),
            dma((n, 2)),
            dma((pieces,)),
            dma((pieces,)),
            dma((pieces,)),
            dma((pieces,)),
            dma((pieces, 2)),
            dma((pieces, 2)),
            dma((2,)),
            dma((2,)),
            dma(()),
            dma(()),
            pltpu.SemaphoreType.REGULAR,
            pltpu.SemaphoreType.REGULAR,
            pltpu.SemaphoreType.REGULAR,
            pltpu.SemaphoreType.REGULAR,
            dma((12,)),
        ],
        compiler_params=pltpu.CompilerParams(
            collective_id=0, has_side_effects=True, vmem_limit_bytes=67043328
        ),
    )(
        query, keys, values, m_x, m_z, m_b, m_c, dt_raw.T,
        dt_bias.reshape(1, -1), a_log.reshape(1, -1), d_skip.reshape(1, -1), norm_gain.reshape(1, -1),
    )


def solution(mesh):
    rows = P(("grp", "ctx"), "hd")
    in_specs = (rows,) * 8 + (P("hd"),) * 4
    return jax.shard_map(
        functools.partial(body, mesh.shape["ctx"], mesh.shape["hd"]),
        mesh=mesh, in_specs=in_specs, out_specs=(rows, rows), check_vma=False,
    )
```

time: 51.6 us -> 46.4 us (0.90)
  the two profiles are of different devices: /device:TPU:8 before, /device:TPU:26 now
where the time goes in v2:
time: 46.4 us; the launch traced here: 46.2 us
  Pallas kernels  43 us (93%)
  local copies, waits for them, and re-layouts  2.52 us (5%)
  between operations  0.65 us (1%)
    pallas_call x1, Pallas kernels, body(): pl.pallas_call(functools.partial(kernel, n, wide_hd), out_shape=(jax.Shap...  43 us
    unnamed x4, local copies, waits for them, and re-layouts  2.52 us

profile of v2, /device:TPU:26, one launch (start us, length us, event | category | flops | bytes accessed | tf_op | source)
XLA Modules:
  0.0 46.2 jit_solution(2576307570890275724)
XLA Ops:
  0.6 43.0 %shard_map.131 = (bf16[128,1024]{1,0:T(8,128)(2,1)}, bf16[128,2048]{1,0:T(8,128)(2,1)}) custom-call(bf16[128,1024]{1,0:T(8,128)(2,1)} %q_in.1, bf16[128,256]{1,0:T(8,128)(2,1)} %k_in.1, bf16[128,256]{1,0:T(8,128)(2,1)} %v_in.1, bf16[128,2048]{1,0:T(8,128)(2,1)} %x_in.1, bf16[128,2048]{1,0:T(8,128)(2,1)} %z_in.1, bf16[128,256]{1,0:T(8,128)(2,1)} %b_in.1, ...), custom_call_target="tpu_custom_call" | custom-call | tf_op jit(solution)/shard_map/pallas_call | solution.py:616
  43.6 0.0 copy-start
  43.6 1.7 %copy.16 = bf16[128,1024]{1,0:T(8,128)(2,1)} copy(bf16[128,1024]{1,0:T(8,128)(2,1)} %get-tuple-element.4) | data formatting | bytes 524288
  45.4 0.0 copy-done
  45.4 0.8 %copy.17 = bf16[128,2048]{1,0:T(8,128)(2,1)} copy(bf16[128,2048]{1,0:T(8,128)(2,1)S(1)} %copy-done) | data formatting | bytes 1048576
Async XLA Ops:
  43.6 1.7 %copy-start = (bf16[128,2048]{1,0:T(8,128)(2,1)S(1)}, bf16[128,2048]{1,0:T(8,128)(2,1)}, u32[]{:S(2)}) copy-start(bf16[128,2048]{1,0:T(8,128)(2,1)} %get-tuple-element.5) | copy-start | bytes 1572868

commit v3 on v2

--- a/solution.py
+++ b/solution.py
@@ -18,6 +18,7 @@
 BF16 = jnp.bfloat16
 INPUT_SPACE = pltpu.HBM
 PIECE = 256
+VMEM_BYTES = 67043328
 
 
 def dot(a, b, ca=1, cb=0, precision=None):
@@ -35,9 +36,9 @@
 
 def kernel(
     n, wide_hd, q_in, k_in, v_in, x_in, z_in, b_in, c_in, dt_in, bias_in, alog_in, skip_in,
-    gain_in, ctx_out, mix_out,
-    q_ref, x_ref, z_ref, b_ref, c_ref, dt_ref, bias_ref, alog_ref, skip_ref, gain_ref,
-    kv_all, bias_scr, ctx_stage, arrived, gated, base_scr, er_scr, xdt_scr, hs, run_split, gmask,
+    gain_in, ctx_out, arrived, gain_ref,
+    q_ref, x_ref, z_ref, b_ref, c_ref, dt_ref, bias_ref, alog_ref, skip_ref,
+    kv_all, bias_scr, ctx_stage, gated, base_scr, er_scr, xdt_scr, hs, run_split, gmask,
     buf_a, buf_b, out_a, out_b, sloc_a, sloc_b, tot_a, tot_b, log_in, log_out, wide_t,
     kv_plus, kv_minus, kv_recv, a_send, a_recv, b_send, b_recv, o_send, o_recv, c_send, c_recv,
     log_send, log_recv, plus_sem, minus_sem, pair_plus, pair_minus, load_sem,
@@ -588,15 +589,30 @@
 
     settle(ctx_stage, ctx_out, slice(None), c_send, c_recv)
     loads[11].wait()
+    for k in range(pieces):
+        settle(gated, arrived, pl.ds(k * piece, piece), o_send.at[k], o_recv.at[k])
+
+
+def finish(groups, ctx_ref, gated_ref, gain_ref, ctx_out, mix_out, mixed, sems):
+    tok, width = gated_ref.shape
+    group_width = width // groups
+    half = tok // 2
+    copies = [pltpu.make_async_copy(ctx_ref, ctx_out, sems.at[0])]
+    copies[0].start()
     for g in range(groups):
-        gcols = slice(g * group_width, (g + 1) * group_width)
-        for k in range(g * per_group, (g + 1) * per_group):
-            settle(gated, arrived, pl.ds(k * piece, piece), o_send.at[k], o_recv.at[k])
         for which in range(2):
-            rows = pl.ds(which * half, half)
-            value = arrived[rows, gcols].astype(F32)
+            rows, cols = pl.ds(which * half, half), pl.ds(g * group_width, group_width)
+            value = gated_ref[rows, cols].astype(F32)
             power = jnp.mean(value * value, axis=-1, keepdims=True)
-            mix_out[rows, gcols] = (value * lax.rsqrt(power + NORM_EPS) * gain_ref[:, gcols]).astype(BF16)
+            mixed[rows, cols] = (value * lax.rsqrt(power + NORM_EPS) * gain_ref[:, cols]).astype(BF16)
+            copies.append(
+                pltpu.make_async_copy(
+                    mixed.at[rows, cols], mix_out.at[rows, cols], sems.at[1 + 2 * g + which]
+                )
+            )
+            copies[-1].start()
+    for copy in copies:
+        copy.wait()
 
 
 def body(n, wide_hd, query, keys, values, m_x, m_z, m_b, m_c, dt_raw, dt_bias, a_log, d_skip, norm_gain):
@@ -613,14 +629,16 @@
     vmem = pltpu.VMEM
     state = (pieces, MN, piece)
     spec = pl.BlockSpec(memory_space=pltpu.VMEM)
-    return pl.pallas_call(
+    spare = 2 * (query.size + m_x.size) + 4 * width + 49152
+    context, gated, gain = pl.pallas_call(
         functools.partial(kernel, n, wide_hd),
         out_shape=(
-            jax.ShapeDtypeStruct(query.shape, BF16),
-            jax.ShapeDtypeStruct(m_x.shape, BF16),
+            vmem(query.shape, BF16),
+            vmem(m_x.shape, BF16),
+            vmem((1, width), F32),
         ),
         in_specs=[anywhere] * 12,
-        out_specs=(spec, spec),
+        out_specs=(spec, spec, spec),
         scratch_shapes=[
             vmem(query.shape, BF16),
             vmem(m_x.shape, BF16),
@@ -631,11 +649,9 @@
             vmem((1, heads), F32),
             vmem((1, heads), F32),
             vmem((1, heads), F32),
-            vmem((1, width), F32),
             vmem((n, tok, 2 * kv), BF16),
             vmem((tok, n * tok), F32),
             vmem(query.shape, BF16),
-            vmem(m_x.shape, BF16),
             vmem(m_x.shape, BF16),
             vmem((tok, width), F32),
             vmem((tok, width), F32),
@@ -674,12 +690,23 @@
             dma((12,)),
         ],
         compiler_params=pltpu.CompilerParams(
-            collective_id=0, has_side_effects=True, vmem_limit_bytes=67043328
+            collective_id=0, has_side_effects=True, vmem_limit_bytes=VMEM_BYTES - spare
         ),
     )(
         query, keys, values, m_x, m_z, m_b, m_c, dt_raw.T,
         dt_bias.reshape(1, -1), a_log.reshape(1, -1), d_skip.reshape(1, -1), norm_gain.reshape(1, -1),
     )
+    return pl.pallas_call(
+        functools.partial(finish, groups),
+        out_shape=(
+            jax.ShapeDtypeStruct(query.shape, BF16),
+            jax.ShapeDtypeStruct(m_x.shape, BF16),
+        ),
+        in_specs=[spec] * 3,
+        out_specs=(anywhere, anywhere),
+        scratch_shapes=[vmem(m_x.shape, BF16), dma((1 + 2 * groups,))],
+        compiler_params=pltpu.CompilerParams(vmem_limit_bytes=4 << 20),
+    )(context, gated, gain)
 
 
 def solution(mesh):

time: 46.4 us -> 43.8 us (0.944)
  local copies, waits for them, and re-layouts: 2.52 us -> 0 us
    unnamed x4 -> x0, local copies, waits for them, and re-layouts: 2.52 us -> none
    pallas_call x1 -> x2, Pallas kernels: 43 us -> 43 us  [the longest x1 42 us: body(): pl.pallas_call(functools.partial(kernel, n, wide_hd), out_shape=(vmem(que...]
where the time goes in v3:
time: 43.8 us; the launch traced here: 43.6 us
  Pallas kernels  43 us (98%)
  between operations  0.64 us (1%)
    pallas_call x1, Pallas kernels, body(): pl.pallas_call(functools.partial(kernel, n, wide_hd), out_shape=(vmem(que...  42 us
    pallas_call x1, Pallas kernels, body(): pl.pallas_call(functools.partial(finish, groups), out_shape=(jax.ShapeDty...  0.96 us

profile of v3, /device:TPU:26, one launch (start us, length us, event | category | flops | bytes accessed | tf_op | source)
XLA Modules:
  0.0 43.6 jit_solution(9195639484221937959)
XLA Ops:
  0.6 42.0 %shard_map.131 = (bf16[128,1024]{1,0:T(8,128)(2,1)S(1)}, bf16[128,2048]{1,0:T(8,128)(2,1)S(1)}, f32[1,2048]{1,0:T(1,128)S(1)}) custom-call(bf16[128,1024]{1,0:T(8,128)(2,1)} %q_in.1, bf16[128,256]{1,0:T(8,128)(2,1)} %k_in.1, bf16[128,256]{1,0:T(8,128)(2,1)} %v_in.1, bf16[128,2048]{1,0:T(8,128)(2,1)} %x_in.1, bf16[128,2048]{1,0:T(8,128)(2,1)} %z_in.1, ...), custom_call_target="tpu_custom_call" | custom-call | tf_op jit(solution)/shard_map/pallas_call | solution.py:633
  42.7 1.0 %shard_map.132 = (bf16[128,1024]{1,0:T(8,128)(2,1)}, bf16[128,2048]{1,0:T(8,128)(2,1)}) custom-call(bf16[128,1024]{1,0:T(8,128)(2,1)S(1)} %get-tuple-element.5.ctx_ref, bf16[128,2048]{1,0:T(8,128)(2,1)S(1)} %get-tuple-element.6.gated_ref, f32[1,2048]{1,0:T(1,128)S(1)} %get-tuple-element.7.gain_ref), custom_call_target="tpu_custom_call" | custom-call | tf_op jit(solution)/shard_map/pallas_call | solution.py:699

commit v4 on v3

--- a/solution.py
+++ b/solution.py
@@ -17,7 +17,8 @@
 F32 = jnp.float32
 BF16 = jnp.bfloat16
 INPUT_SPACE = pltpu.HBM
-PIECE = 256
+PIECE = 128
+UNIT = 256
 VMEM_BYTES = 67043328
 
 
@@ -51,8 +52,11 @@
     groups = b_ref.shape[1] // MN
     group_width = width // groups
     pieces, _, piece = buf_a.shape
-    per_piece = piece // MP
-    per_group = group_width // piece
+    units = o_send.shape[0]
+    unit = width // units
+    per_unit = unit // MP
+    per_group = group_width // unit
+    span = unit // piece
     q_heads = q_ref.shape[1] // HEAD_SIZE
     kv = kv_all.shape[2] // 2
     repeat = q_ref.shape[1] // kv
@@ -74,24 +78,24 @@
             )
         )
     ]
+    barrier = pltpu.get_barrier_semaphore()
+
+    def greet(peer):
+        pl.semaphore_signal(barrier, inc=1, device_id={"ctx": peer}, device_id_type=mesh_id)
+
+    @pl.when(has_left)
+    def _():
+        greet(me - 1)
+
+    @pl.when(has_right)
+    def _():
+        greet(me + 1)
+
+    if paired:
+        pl.semaphore_signal(barrier, inc=1, device_id={"hd": partner}, device_id_type=mesh_id)
+
     for load in loads:
         load.start()
-
-    barrier = pltpu.get_barrier_semaphore()
-
-    def greet(peer):
-        pl.semaphore_signal(barrier, inc=1, device_id={"ctx": peer}, device_id_type=mesh_id)
-
-    @pl.when(has_left)
-    def _():
-        greet(me - 1)
-
-    @pl.when(has_right)
-    def _():
-        greet(me + 1)
-
-    if paired:
-        pl.semaphore_signal(barrier, inc=1, device_id={"hd": partner}, device_id_type=mesh_id)
 
     def remote(src, dst, send, recv, peer):
         return pltpu.make_async_remote_copy(
@@ -146,22 +150,9 @@
     for load in loads[4:6]:
         load.wait()
 
-    pl.semaphore_wait(barrier, has_left.astype(jnp.int32) + has_right.astype(jnp.int32) + int(paired))
-
-    @pl.when(jnp.logical_not(has_right))
-    def _():
-        log_out[...] = own_log
-        log_copy().start()
-
-    @pl.when(has_right & has_left)
-    def _():
-        kv_right(me).start()
-        for copy in kv_left(me):
-            copy.start()
-
     for load in loads[6:8]:
         load.wait()
-    lanes = per_piece * half
+    lanes = per_unit * half
     lane = lax.broadcasted_iota(jnp.int32, (half, lanes), 1)
     source = lane - lane // half * half
     target = lax.broadcasted_iota(jnp.int32, (half, lanes), 0)
@@ -171,7 +162,7 @@
         cols = slice(g * MN, (g + 1) * MN)
         for which in range(2):
             rows = slice(which * half, (which + 1) * half)
-            repeated = jnp.concatenate([b_ref[rows, cols]] * per_piece, axis=0)
+            repeated = jnp.concatenate([b_ref[rows, cols]] * per_unit, axis=0)
             gmask[g, rows, :] = jnp.where(causal, dot(c_ref[rows, cols], repeated, 1, 1), 0.0)
 
     @pl.when(me == 0)
@@ -183,11 +174,11 @@
         buf_b[...] = jnp.zeros_like(buf_b)
         wide_t[...] = jnp.ones_like(wide_t)
 
-    split_head = lax.rem(lax.broadcasted_iota(jnp.int32, (3 * heads, piece), 0), heads)
-    lane_head = lax.broadcasted_iota(jnp.int32, (3 * heads, piece), 1) // MP
+    split_head = lax.rem(lax.broadcasted_iota(jnp.int32, (3 * heads, unit), 0), heads)
+    lane_head = lax.broadcasted_iota(jnp.int32, (3 * heads, unit), 1) // MP
     wide_head = lax.rem(lax.broadcasted_iota(jnp.int32, (3 * heads, lanes), 0), heads)
     wide_lane = lax.broadcasted_iota(jnp.int32, (3 * heads, lanes), 1) // half
-    part_head = lax.broadcasted_iota(jnp.int32, (half, piece), 1) // MP
+    part_head = lax.broadcasted_iota(jnp.int32, (half, unit), 1) // MP
 
     def block_id(which):
         return me if which == 0 else 2 * n - 1 - me
@@ -212,23 +203,27 @@
         return value / (1.0 + jnp.exp(-value))
 
     def prepare(k):
-        cols = pl.ds(pl.multiple_of(k * piece, piece), piece)
+        cols = pl.ds(pl.multiple_of(k * unit, unit), unit)
         gcols = pl.ds(pl.multiple_of((k // per_group) * MN, MN), MN)
-        spread = dot(hs[...], (split_head == k * per_piece + lane_head).astype(BF16))
+        spread = dot(hs[...], (split_head == k * per_unit + lane_head).astype(BF16))
         xs = x_ref[:, cols].astype(F32)
         weighted = (xs * spread[tok : 2 * tok]).astype(BF16)
         b_rows = b_ref[:, gcols]
-        sloc_a[k] = dot(b_rows[0:half], weighted[0:half], 0, 0)
-        sloc_b[k] = dot(b_rows[half:], weighted[half:], 0, 0)
-        tot_a[k] = jnp.broadcast_to(spread[half - 1 : half], (8, piece))
-        tot_b[k] = jnp.broadcast_to(spread[tok - 1 : tok], (8, piece))
+        local_a = dot(b_rows[0:half], weighted[0:half], 0, 0)
+        local_b = dot(b_rows[half:], weighted[half:], 0, 0)
+        for i in range(span):
+            part = slice(i * piece, (i + 1) * piece)
+            sloc_a[span * k + i] = local_a[:, part]
+            sloc_b[span * k + i] = local_b[:, part]
+            tot_a[span * k + i] = jnp.broadcast_to(spread[half - 1 : half, part], (8, piece))
+            tot_b[span * k + i] = jnp.broadcast_to(spread[tok - 1 : tok, part], (8, piece))
         er_scr[:, cols] = spread[0:tok]
         xdt_scr[:, cols] = (xs * spread[2 * tok : 3 * tok]).astype(BF16)
         base_scr[:, cols] = spread[3 * tok : 3 * tok + 1] * xs
 
     def within_blocks(k):
-        cols = pl.ds(pl.multiple_of(k * piece, piece), piece)
-        wide = dot(run_split[...], (wide_head == k * per_piece + wide_lane).astype(BF16))
+        cols = pl.ds(pl.multiple_of(k * unit, unit), unit)
+        wide = dot(run_split[...], (wide_head == k * per_unit + wide_lane).astype(BF16))
         for which in range(2):
             rows = slice(which * half, (which + 1) * half)
             mine = wide[rows]
@@ -237,7 +232,7 @@
             part = xdt_scr[rows, cols]
             none = jnp.zeros_like(part)
             stacked = jnp.concatenate(
-                [jnp.where(part_head == h, part, none) for h in range(per_piece)], axis=0
+                [jnp.where(part_head == h, part, none) for h in range(per_unit)], axis=0
             )
             base_scr[rows, cols] = base_scr[rows, cols] + dot(weights, stacked)
 
@@ -271,27 +266,28 @@
             b_copy(k).start()
 
     def gate(k, which, state):
-        cols = pl.ds(pl.multiple_of(k * piece, piece), piece)
+        cols = pl.ds(pl.multiple_of(k * unit, unit), unit)
         gcols = pl.ds(pl.multiple_of((k // per_group) * MN, MN), MN)
         rows = slice(which * half, (which + 1) * half)
         carried = dot(c_ref[rows, gcols], state) * er_scr[rows, cols]
         z = z_ref[rows, cols].astype(F32)
-        value = ((base_scr[rows, cols] + carried) * silu(z)).astype(BF16)
-        gated[rows, cols] = value
-
-    def send_gated(k):
-        cols = pl.ds(pl.multiple_of(k * piece, piece), piece)
-        for which in range(2):
-            send(gated, arrived, cols, o_send.at[k], o_recv.at[k], which)
+        gated[rows, cols] = ((base_scr[rows, cols] + carried) * silu(z)).astype(BF16)
+
+    def send_gated(k, which):
+        cols = pl.ds(pl.multiple_of(k * unit, unit), unit)
+        send(gated, arrived, cols, o_send.at[k], o_recv.at[k], which)
 
     def gate_a(k):
-        gate(k, 0, buf_a[k])
+        gate(k, 0, jnp.concatenate([buf_a[span * k + i] for i in range(span)], axis=1))
 
     def gate_b(k):
-        cols = pl.ds(pl.multiple_of(k * piece, piece), piece)
-        after = buf_a[k].astype(F32) * tot_a[k][0:1] + sloc_a[k]
-        entering = after * wide_t[0:1, cols] + buf_b[k].astype(F32)
-        gate(k, 1, entering.astype(BF16))
+        entering = []
+        for i in range(span):
+            j = span * k + i
+            cols = pl.ds(pl.multiple_of(j * piece, piece), piece)
+            after = buf_a[j].astype(F32) * tot_a[j][0:1] + sloc_a[j]
+            entering.append((after * wide_t[0:1, cols] + buf_b[j].astype(F32)).astype(BF16))
+        gate(k, 1, jnp.concatenate(entering, axis=1))
 
     def take_log():
         @pl.when(has_right)
@@ -367,72 +363,102 @@
         for which in range(2):
             send(ctx_stage, ctx_out, slice(None), c_send, c_recv, which)
 
-    for load in loads[8:11]:
+    loads[8].wait()
+    hops = n - 1 - me
+    middle = pieces // 2
+
+    peers = has_left.astype(jnp.int32) + has_right.astype(jnp.int32) + int(paired)
+
+    @pl.when(has_left)
+    def _():
+        pl.semaphore_wait(barrier, peers)
+
+    @pl.when(jnp.logical_not(has_right))
+    def _():
+        log_out[...] = own_log
+        log_copy().start()
+
+    @pl.when(has_right & has_left)
+    def _():
+        kv_right(me).start()
+        for copy in kv_left(me):
+            copy.start()
+
+    prepare(0)
+
+    @pl.when(jnp.logical_not(has_left))
+    def _():
+        pl.semaphore_wait(barrier, peers)
+
+    def first_step(k, _):
+        @pl.when(k > 0)
+        def _():
+            prepare(k)
+
+        @pl.when((k == units // 2) & (me == 0))
+        def _():
+            relay_right(0)
+
+        @pl.when((k == units // 2) & (me == n - 1))
+        def _():
+            relay_left(0)
+
+        for i in range(span):
+            @pl.when(me == 0)
+            def _(i=i):
+                step_a(span * k + i)
+
+            @pl.when(me == n - 1)
+            def _(i=i):
+                step_b(span * k + i)
+
+        return 0
+
+    lax.fori_loop(0, units, first_step, 0)
+    for load in loads[9:11]:
         load.wait()
     attention_mask()
-    hops = n - 1 - me
-    middle = pieces // 2
-
-    def first_step(k, _):
-        prepare(k)
-
-        @pl.when((k == middle) & (me == 0))
-        def _():
-            relay_right(0)
-
-        @pl.when((k == middle) & (me == n - 1))
-        def _():
-            relay_left(0)
-
-        @pl.when(me == 0)
-        def _():
-            step_a(k)
-
-        @pl.when(me == n - 1)
-        def _():
-            step_b(k)
-
-        return 0
-
-    lax.fori_loop(0, pieces, first_step, 0)
 
     def base(distance):
-        return (9 * jnp.maximum(distance - 1, 0)) // 4
+        return (14 * jnp.maximum(distance - 1, 0)) // 3
 
     lag_a = base(me)
     lag_b = base(hops)
     block_b = 2 * n - 1 - me
     hold_plus = block_b // 2 - 1 > me
     hold_minus = me // 2 + 1 < me
-    gap = jnp.where(hops > 1, 2, 1)
-    attend = 1 + jnp.maximum(
-        jnp.where(has_left, lag_a + middle, 0), jnp.where(has_right, lag_b + middle + gap, 0)
-    )
-    gates = jnp.maximum(lag_a + middle + 1, lag_b + middle + gap + 1)
-    gates = gates + jnp.where(2 * me < n, jnp.where(has_left, 2, 1), jnp.where(has_right, 3, 1))
-    gates = jnp.maximum(gates, jnp.where(hold_plus, lag_a + pieces + 1, 0))
-    gates = jnp.maximum(gates, jnp.where(hold_minus, lag_b + pieces + gap + 1, 0))
-    place_ctx = jnp.maximum(attend + q_heads // 2 - 1, gates)
+    gap = jnp.where(hops > 1, 6, 2)
+    free = jnp.maximum(lag_a + pieces + 1, lag_b + pieces + gap + 1)
+    gates = jnp.maximum(lag_a, lag_b + gap) + pieces - units + 3
+    gates = gates + jnp.where(2 * me < n, jnp.where(has_left, 3, 0), jnp.where(has_right, 7, 1))
+    gates = jnp.maximum(gates, jnp.where(hold_plus, lag_a + pieces + 2, 0))
+    gates = jnp.maximum(gates, jnp.where(hold_minus, lag_b + pieces + gap + 2, 0))
+    quick = gates >= jnp.maximum(lag_a + pieces + 2, lag_b + pieces + gap + 2)
+    ending = has_left & jnp.logical_not(has_right)
+    first_out = jnp.where((2 * me < n) | jnp.logical_not(has_right), 1, 0)
+    early = lag_b + middle + 1
+    fills = has_left & has_right & (2 * me >= n) & (lag_a + 2 * span <= early)
     last = functools.reduce(jnp.maximum, [
-        lag_a + pieces + 2, lag_b + pieces + gap + 2, attend + q_heads // 2, place_ctx + 1,
-        gates + middle, 3 * n,
+        lag_a + pieces + 2, lag_b + pieces + gap + 2, gates + jnp.where(quick, middle // 2, middle),
+        6 * n - 10, 2 * units,
     ])
 
-    def passed(pair_sem, sem, peers, wait):
-        any_peer = functools.reduce(jnp.logical_or, [ok for _, ok in peers])
-
-        @pl.when(any_peer)
-        def _():
-            if paired and not wait:
+    def greet_pair(pair_sem, peers):
+        if paired:
+            @pl.when(functools.reduce(jnp.logical_or, [ok for _, ok in peers]))
+            def _():
                 pl.semaphore_signal(pair_sem, inc=1, device_id={"hd": partner}, device_id_type=mesh_id)
-            elif paired:
+
+    def release(pair_sem, sem, peers):
+        if paired:
+            @pl.when(functools.reduce(jnp.logical_or, [ok for _, ok in peers]))
+            def _():
                 pl.semaphore_wait(pair_sem, 1)
 
-        if wait:
-            for peer, ok in peers:
-                @pl.when(ok)
-                def _(peer=peer):
-                    pl.semaphore_signal(sem, inc=1, device_id={"ctx": peer}, device_id_type=mesh_id)
+        for peer, ok in peers:
+            @pl.when(ok)
+            def _(peer=peer):
+                pl.semaphore_signal(sem, inc=1, device_id={"ctx": peer}, device_id_type=mesh_id)
 
     plus_peers = [(p, (p >= 0) & (p < me)) for p in (2 * n - 3 - 2 * me, 2 * n - 4 - 2 * me)]
     minus_peers = [(p, (p > me) & (p < n)) for p in (2 * me - 2, 2 * me - 1)]
@@ -446,19 +472,15 @@
         def _():
             relay_right(me)
 
-        k = jnp.where(at < middle, at, at - 1)
-
-        @pl.when((at >= 0) & (at <= pieces) & (at != middle) & has_left)
+        k = jnp.where(at < middle, at, at - 2)
+
+        @pl.when(((at >= 0) & (at < middle) | (at > middle + 1) & (at < pieces + 2)) & has_left)
         def _():
             step_a(k)
 
-        @pl.when((at == pieces) & has_left)
-        def _():
-            passed(pair_plus, plus_sem, plus_peers, False)
-
         @pl.when((at == pieces + 1) & has_left)
         def _():
-            passed(pair_plus, plus_sem, plus_peers, True)
+            greet_pair(pair_plus, plus_peers)
 
     def chain_b(t):
         at = t - lag_b
@@ -471,19 +493,15 @@
         def _():
             relay_left(hops)
 
-        k = jnp.where(at < middle, at, at - gap - 1)
-
-        @pl.when(((at >= 0) & (at < middle) | (at > middle + gap) & (at <= pieces + gap)) & has_right)
+        k = jnp.where(at < middle, at, at - gap - 2)
+
+        @pl.when(((at >= 0) & (at < middle) | (at > middle + gap + 1) & (at <= pieces + gap + 1)) & has_right)
         def _():
             step_b(k)
 
-        @pl.when((at == pieces + gap) & has_right)
-        def _():
-            passed(pair_minus, minus_sem, minus_peers, False)
-
         @pl.when((at == pieces + gap + 1) & has_right)
         def _():
-            passed(pair_minus, minus_sem, minus_peers, True)
+            greet_pair(pair_minus, minus_peers)
 
     def slot_step(t, _):
         @pl.when(2 * me >= n)
@@ -496,23 +514,23 @@
         def _():
             chain_b(t)
 
+        @pl.when(t == free)
+        def _():
+            release(pair_minus, minus_sem, minus_peers)
+            release(pair_plus, plus_sem, plus_peers)
+
         for h in range(1, n - 1):
-            @pl.when((t == 2 * h - 2) & (h < me))
+            @pl.when((t == 4 * h - 4) & (h < me))
             def _(h=h):
                 relay_right(h)
 
-            @pl.when((t == 3 * h - 2) & (h < hops))
+            @pl.when((t == 6 * h - 4) & (h < hops))
             def _(h=h):
                 relay_left(h)
 
-        @pl.when(t < pieces)
-        def _():
-            within_blocks(t)
-
-        @pl.when((t >= attend) & (t < attend + q_heads // 2))
-        def _():
-            one_head(2 * (t - attend))
-            one_head(2 * (t - attend) + 1)
+        @pl.when((t < 2 * units) & (lax.rem(t, 2) == 0))
+        def _():
+            within_blocks(t // 2)
 
         @pl.when((t == gates) & hold_plus)
         def _():
@@ -522,21 +540,65 @@
         def _():
             pl.semaphore_wait(minus_sem, 1)
 
-        @pl.when(t == place_ctx)
-        def _():
-            send_ctx()
-
-        @pl.when((t >= gates) & (t < gates + middle))
+        @pl.when((t == early) & fills)
         def _():
             for i in range(2):
-                gate_a(2 * (t - gates) + i)
-                gate_b(2 * (t - gates) + i)
+                gate_a(i)
             for i in range(2):
-                send_gated(2 * (t - gates) + i)
+                send_gated(i, 0)
+
+        @pl.when((t == lag_a + middle - 1) & ending)
+        def _():
+            def gate_early(i, _):
+                for j in range(2):
+                    gate_a(2 * i + j)
+                    gate_b(2 * i + j)
+                for j in range(2):
+                    send_gated(2 * i + j, 1)
+                return 0
+
+            lax.fori_loop(0, units // 4, gate_early, 0)
+
+        at = jnp.where(quick, 2, 1) * (t - gates)
+        on = (at >= jnp.where(ending, units // 4 * 2, 0)) & (at < units) & (lax.rem(at, 2) == 0)
+        done_a = fills & (at == 0)
+
+        @pl.when(on & jnp.logical_not(done_a))
+        def _():
+            for i in range(2):
+                gate_a(at + i)
+                gate_b(at + i)
+            for which in range(2):
+                @pl.when(first_out == which)
+                def _(which=which):
+                    for i in range(2):
+                        send_gated(at + i, which)
+
+        @pl.when(on & done_a)
+        def _():
+            for i in range(2):
+                gate_b(at + i)
 
         return 0
 
     lax.fori_loop(0, last, slot_step, 0)
+
+    for which in range(2):
+        @pl.when(first_out != which)
+        def _(which=which):
+            def send_rest(k, _):
+                send_gated(k, which)
+                return 0
+
+            lax.fori_loop(0, units, send_rest, 0)
+
+    def two_heads(i, _):
+        one_head(2 * i)
+        one_head(2 * i + 1)
+        return 0
+
+    lax.fori_loop(0, q_heads // 2, two_heads, 0)
+    send_ctx()
 
     def drain(k, _):
         @pl.when(has_right)
@@ -589,8 +651,8 @@
 
     settle(ctx_stage, ctx_out, slice(None), c_send, c_recv)
     loads[11].wait()
-    for k in range(pieces):
-        settle(gated, arrived, pl.ds(k * piece, piece), o_send.at[k], o_recv.at[k])
+    for k in range(units):
+        settle(gated, arrived, pl.ds(k * unit, unit), o_send.at[k], o_recv.at[k])
 
 
 def finish(groups, ctx_ref, gated_ref, gain_ref, ctx_out, mix_out, mixed, sems):
@@ -623,6 +685,8 @@
     groups = m_b.shape[1] // MN
     piece = math.gcd(width // groups, PIECE)
     pieces = width // piece
+    unit = math.gcd(width // groups, UNIT)
+    units = width // unit
     kv = keys.shape[1]
     q_heads = query.shape[1] // HEAD_SIZE
     dma = pltpu.SemaphoreType.DMA
@@ -658,7 +722,7 @@
             vmem((tok, width), BF16),
             vmem((3 * tok + 16, 3 * heads), BF16),
             vmem((tok, 3 * heads), BF16),
-            vmem((groups, tok, piece // MP * (tok // 2)), F32),
+            vmem((groups, tok, unit // MP * (tok // 2)), F32),
             vmem(state, BF16),
             vmem(state, BF16),
             vmem(state, BF16),
@@ -677,8 +741,8 @@
             dma((pieces,)),
             dma((pieces,)),
             dma((pieces,)),
-            dma((pieces, 2)),
-            dma((pieces, 2)),
+            dma((units, 2)),
+            dma((units, 2)),
             dma((2,)),
             dma((2,)),
             dma(()),

time: 43.8 us -> 43 us (0.982)
  Pallas kernels: 43 us -> 42.2 us
    pallas_call x1, Pallas kernels: 42 us -> 41.2 us  [body(): pl.pallas_call(functools.partial(kernel, n, wide_hd), out_shape=(vmem(que...]
where the time goes in v4:
time: 43 us; the launch traced here: 42.8 us
  Pallas kernels  42.2 us (98%)
  between operations  0.64 us (1%)
    pallas_call x1, Pallas kernels, body(): pl.pallas_call(functools.partial(kernel, n, wide_hd), out_shape=(vmem(que...  41.2 us
    pallas_call x1, Pallas kernels, body(): pl.pallas_call(functools.partial(finish, groups), out_shape=(jax.ShapeDty...  0.96 us

profile of v4, /device:TPU:26, one launch (start us, length us, event | category | flops | bytes accessed | tf_op | source)
XLA Modules:
  0.0 42.8 jit_solution(17948505331888121207)
XLA Ops:
  0.6 41.2 %shard_map.131 = (bf16[128,1024]{1,0:T(8,128)(2,1)S(1)}, bf16[128,2048]{1,0:T(8,128)(2,1)S(1)}, f32[1,2048]{1,0:T(1,128)S(1)}) custom-call(bf16[128,1024]{1,0:T(8,128)(2,1)} %q_in.1, bf16[128,256]{1,0:T(8,128)(2,1)} %k_in.1, bf16[128,256]{1,0:T(8,128)(2,1)} %v_in.1, bf16[128,2048]{1,0:T(8,128)(2,1)} %x_in.1, bf16[128,2048]{1,0:T(8,128)(2,1)} %z_in.1, ...), custom_call_target="tpu_custom_call" | custom-call | tf_op jit(solution)/shard_map/pallas_call | solution.py:697
  41.9 1.0 %shard_map.132 = (bf16[128,1024]{1,0:T(8,128)(2,1)}, bf16[128,2048]{1,0:T(8,128)(2,1)}) custom-call(bf16[128,1024]{1,0:T(8,128)(2,1)S(1)} %get-tuple-element.5.ctx_ref, bf16[128,2048]{1,0:T(8,128)(2,1)S(1)} %get-tuple-element.6.gated_ref, f32[1,2048]{1,0:T(1,128)S(1)} %get-tuple-element.7.gain_ref), custom_call_target="tpu_custom_call" | custom-call | tf_op jit(solution)/shard_map/pallas_call | solution.py:763

commit v5 on v4

--- a/solution.py
+++ b/solution.py
@@ -38,7 +38,7 @@
 def kernel(
     n, wide_hd, q_in, k_in, v_in, x_in, z_in, b_in, c_in, dt_in, bias_in, alog_in, skip_in,
     gain_in, ctx_out, arrived, gain_ref,
-    q_ref, x_ref, z_ref, b_ref, c_ref, dt_ref, bias_ref, alog_ref, skip_ref,
+    q_ref, x_ref, z_ref, bc_ref, dt_ref, small_ref,
     kv_all, bias_scr, ctx_stage, gated, base_scr, er_scr, xdt_scr, hs, run_split, gmask,
     buf_a, buf_b, out_a, out_b, sloc_a, sloc_b, tot_a, tot_b, log_in, log_out, wide_t,
     kv_plus, kv_minus, kv_recv, a_send, a_recv, b_send, b_recv, o_send, o_recv, c_send, c_recv,
@@ -49,11 +49,11 @@
     half = tok // 2
     heads = dt_ref.shape[0]
     width = x_ref.shape[1]
-    groups = b_ref.shape[1] // MN
+    groups = bc_ref.shape[2] // MN
     group_width = width // groups
     pieces, _, piece = buf_a.shape
-    units = o_send.shape[0]
-    unit = width // units
+    unit = math.gcd(group_width, UNIT)
+    units = width // unit
     per_unit = unit // MP
     per_group = group_width // unit
     span = unit // piece
@@ -67,17 +67,20 @@
     has_left = me > 0
     has_right = me < n - 1
 
+    b_ref, c_ref = bc_ref.at[0], bc_ref.at[1]
+    bias_ref, alog_ref, skip_ref = (small_ref.at[i] for i in range(3))
+    parts = (
+        ((dt_in, dt_ref),),
+        ((bias_in, bias_ref), (alog_in, alog_ref), (skip_in, skip_ref)),
+        ((k_in, kv_all.at[me, :, pl.ds(0, kv)]), (v_in, kv_all.at[me, :, pl.ds(kv, kv)])),
+        ((b_in, b_ref), (c_in, c_ref)), ((x_in, x_ref),), ((z_in, z_ref),), ((q_in, q_ref),),
+        ((gain_in, gain_ref),),
+    )
+    wholes = (dt_ref, small_ref, kv_all.at[me], bc_ref, x_ref, z_ref, q_ref, gain_ref)
     loads = [
-        pltpu.make_async_copy(src, dst, load_sem.at[i])
-        for i, (src, dst) in enumerate(
-            (
-                (dt_in, dt_ref), (bias_in, bias_ref), (alog_in, alog_ref), (skip_in, skip_ref),
-                (k_in, kv_all.at[me, :, pl.ds(0, kv)]), (v_in, kv_all.at[me, :, pl.ds(kv, kv)]),
-                (b_in, b_ref), (c_in, c_ref), (x_in, x_ref), (z_in, z_ref), (q_in, q_ref),
-                (gain_in, gain_ref),
-            )
-        )
+        pltpu.make_async_copy(whole, whole, load_sem.at[i]) for i, whole in enumerate(wholes)
     ]
+
     barrier = pltpu.get_barrier_semaphore()
 
     def greet(peer):
@@ -94,8 +97,9 @@
     if paired:
         pl.semaphore_signal(barrier, inc=1, device_id={"hd": partner}, device_id_type=mesh_id)
 
-    for load in loads:
-        load.start()
+    for i, pairs in enumerate(parts):
+        for src, dst in pairs:
+            pltpu.make_async_copy(src, dst, load_sem.at[i]).start()
 
     def remote(src, dst, send, recv, peer):
         return pltpu.make_async_remote_copy(
@@ -107,14 +111,14 @@
 
     def kv_right(s):
         part = kv_all.at[s, first]
-        return remote(part, part, kv_plus.at[s], kv_recv.at[s, 0], jnp.minimum(me + 1, n - 1))
+        return remote(part, part, kv_plus, kv_recv.at[s, 0], jnp.minimum(me + 1, n - 1))
 
     def kv_left(s):
         copies = []
         for i in range(2):
             part = kv_all.at[s, pl.ds(i * half, half)]
             copies.append(
-                remote(part, part, kv_minus.at[s, i], kv_recv.at[s, i], jnp.maximum(me - 1, 0))
+                remote(part, part, kv_minus, kv_recv.at[s, i], jnp.maximum(me - 1, 0))
             )
         return copies
 
@@ -123,7 +127,7 @@
 
     row = lax.broadcasted_iota(jnp.int32, (tok, tok), 0)
     col = lax.broadcasted_iota(jnp.int32, (tok, tok), 1)
-    for load in loads[:4]:
+    for load in loads[:2]:
         load.wait()
     raw = dot((row == col).astype(BF16), dt_ref[...], 1, 1) + bias_ref[...]
     steps = jnp.maximum(raw, 0.0) + jnp.log1p(jnp.exp(-jnp.abs(raw)))
@@ -147,10 +151,7 @@
     keep_split(hs, 3 * tok, jnp.broadcast_to(skip_ref[...], (16, heads)))
     own_log = jnp.broadcast_to(run[half - 1 : half] + run[tok - 1 : tok], (8, heads))
 
-    for load in loads[4:6]:
-        load.wait()
-
-    for load in loads[6:8]:
+    for load in loads[2:4]:
         load.wait()
     lanes = per_unit * half
     lane = lax.broadcasted_iota(jnp.int32, (half, lanes), 1)
@@ -196,7 +197,7 @@
         @pl.when(owner != me)
         def _():
             remote(
-                stage.at[rows, cols], final.at[target, cols], send_sem.at[which], recv_sem.at[slot], owner
+                stage.at[rows, cols], final.at[target, cols], send_sem, recv_sem, owner
             ).start()
 
     def silu(value):
@@ -237,10 +238,10 @@
             base_scr[rows, cols] = base_scr[rows, cols] + dot(weights, stacked)
 
     def a_copy(k):
-        return remote(out_a.at[k], buf_a.at[k], a_send.at[k], a_recv.at[k], jnp.minimum(me + 1, n - 1))
+        return remote(out_a.at[k], buf_a.at[k], a_send, a_recv.at[k], jnp.minimum(me + 1, n - 1))
 
     def b_copy(k):
-        return remote(out_b.at[k], buf_b.at[k], b_send.at[k], b_recv.at[k], jnp.maximum(me - 1, 0))
+        return remote(out_b.at[k], buf_b.at[k], b_send, b_recv.at[k], jnp.maximum(me - 1, 0))
 
     def step_a(k):
         @pl.when(has_left)
@@ -275,7 +276,7 @@
 
     def send_gated(k, which):
         cols = pl.ds(pl.multiple_of(k * unit, unit), unit)
-        send(gated, arrived, cols, o_send.at[k], o_recv.at[k], which)
+        send(gated, arrived, cols, o_send, o_recv, which)
 
     def gate_a(k):
         gate(k, 0, jnp.concatenate([buf_a[span * k + i] for i in range(span)], axis=1))
@@ -363,7 +364,7 @@
         for which in range(2):
             send(ctx_stage, ctx_out, slice(None), c_send, c_recv, which)
 
-    loads[8].wait()
+    loads[4].wait()
     hops = n - 1 - me
     middle = pieces // 2
 
@@ -415,7 +416,7 @@
         return 0
 
     lax.fori_loop(0, units, first_step, 0)
-    for load in loads[9:11]:
+    for load in loads[5:7]:
         load.wait()
     attention_mask()
 
@@ -600,59 +601,46 @@
     lax.fori_loop(0, q_heads // 2, two_heads, 0)
     send_ctx()
 
-    def drain(k, _):
-        @pl.when(has_right)
-        def _():
-            a_copy(k).wait_send()
-
-        @pl.when(has_left)
-        def _():
-            b_copy(k).wait_send()
-
-        return 0
-
-    lax.fori_loop(0, pieces, drain, 0)
+    @pl.when(has_right)
+    def _():
+        remote(out_a, buf_a, a_send, a_recv.at[0], me).wait_send()
 
     @pl.when(has_left)
     def _():
+        remote(out_b, buf_b, b_send, b_recv.at[0], me).wait_send()
+
+    @pl.when(has_left)
+    def _():
         log_copy().wait_send()
 
-    def drain_kv(s, _):
-        @pl.when((s <= me) & has_right)
-        def _():
-            kv_right(s).wait_send()
-
-        @pl.when((s >= me) & has_left)
-        def _():
-            for copy in kv_left(s):
-                copy.wait_send()
-
-        return 0
-
-    lax.fori_loop(0, n, drain_kv, 0)
-
-    def settle(stage, final, cols, send_sem, recv_sem):
-        for which in range(2):
-            rows = pl.ds(which * half, half)
-            copy = remote(stage.at[rows, cols], final.at[rows, cols], send_sem.at[which], recv_sem.at[which], me)
-
-            @pl.when(block_id(which) // 2 != me)
-            def _():
-                copy.wait_send()
-
-        for slot in range(2):
-            source = jnp.where(2 * me + slot < n, 2 * me + slot, 2 * n - 1 - 2 * me - slot)
-            rows = pl.ds(slot * half, half)
-            copy = remote(stage.at[rows, cols], final.at[rows, cols], send_sem.at[slot], recv_sem.at[slot], me)
-
-            @pl.when(source != me)
-            def _():
-                copy.wait_recv()
-
-    settle(ctx_stage, ctx_out, slice(None), c_send, c_recv)
-    loads[11].wait()
-    for k in range(units):
-        settle(gated, arrived, pl.ds(k * unit, unit), o_send.at[k], o_recv.at[k])
+    for i in range(n):
+        @pl.when((me == i) & has_right)
+        def _(i=i):
+            part = kv_all.at[pl.ds(0, i + 1), first]
+            remote(part, part, kv_plus, kv_recv.at[0, 0], me).wait_send()
+
+        @pl.when((me == i) & has_left)
+        def _(i=i):
+            part = kv_all.at[pl.ds(i, n - i)]
+            remote(part, part, kv_minus, kv_recv.at[0, 0], me).wait_send()
+
+    def settle(stage, final, send_sem, recv_sem):
+        def whole(rows):
+            return remote(stage.at[pl.ds(0, rows)], final.at[pl.ds(0, rows)], send_sem, recv_sem, me)
+
+        kept = (block_id(0) // 2 == me) | (block_id(1) // 2 == me)
+        for rows, here in ((tok, jnp.logical_not(kept)), (half, kept)):
+            @pl.when(here)
+            def _(rows=rows):
+                whole(rows).wait_send()
+
+            @pl.when(here)
+            def _(rows=rows):
+                whole(rows).wait_recv()
+
+    settle(ctx_stage, ctx_out, c_send, c_recv)
+    loads[7].wait()
+    settle(gated, arrived, o_send, o_recv)
 
 
 def finish(groups, ctx_ref, gated_ref, gain_ref, ctx_out, mix_out, mixed, sems):
@@ -707,12 +695,9 @@
             vmem(query.shape, BF16),
             vmem(m_x.shape, BF16),
             vmem(m_x.shape, BF16),
-            vmem(m_b.shape, BF16),
-            vmem(m_b.shape, BF16),
+            vmem((2,) + m_b.shape, BF16),
             vmem((heads, tok), BF16),
-            vmem((1, heads), F32),
-            vmem((1, heads), F32),
-            vmem((1, heads), F32),
+            vmem((3, 1, heads), F32),
             vmem((n, tok, 2 * kv), BF16),
             vmem((tok, n * tok), F32),
             vmem(query.shape, BF16),
@@ -734,24 +719,24 @@
             vmem((8, heads), F32),
             vmem((8, heads), F32),
             vmem((8, width), F32),
-            dma((n,)),
+            dma(()),
+            dma(()),
             dma((n, 2)),
-            dma((n, 2)),
+            dma(()),
             dma((pieces,)),
+            dma(()),
             dma((pieces,)),
-            dma((pieces,)),
-            dma((pieces,)),
-            dma((units, 2)),
-            dma((units, 2)),
-            dma((2,)),
-            dma((2,)),
+            dma(()),
+            dma(()),
+            dma(()),
+            dma(()),
             dma(()),
             dma(()),
             pltpu.SemaphoreType.REGULAR,
             pltpu.SemaphoreType.REGULAR,
             pltpu.SemaphoreType.REGULAR,
             pltpu.SemaphoreType.REGULAR,
-            dma((12,)),
+            dma((8,)),
         ],
         compiler_params=pltpu.CompilerParams(
             collective_id=0, has_side_effects=True, vmem_limit_bytes=VMEM_BYTES - spare

time: 43 us -> 42.3 us (0.984)
  Pallas kernels: 42.2 us -> 41.4 us
    pallas_call x1, Pallas kernels: 41.2 us -> 40.5 us  [body(): pl.pallas_call(functools.partial(kernel, n, wide_hd), out_shape=(vmem(que...]
where the time goes in v5:
time: 42.3 us; the launch traced here: 42.1 us
  Pallas kernels  41.4 us (98%)
  between operations  0.64 us (2%)
    pallas_call x1, Pallas kernels, body(): pl.pallas_call(functools.partial(kernel, n, wide_hd), out_shape=(vmem(que...  40.5 us
    pallas_call x1, Pallas kernels, body(): pl.pallas_call(functools.partial(finish, groups), out_shape=(jax.ShapeDty...  0.96 us

profile of v5, /device:TPU:26, one launch (start us, length us, event | category | flops | bytes accessed | tf_op | source)
XLA Modules:
  0.0 42.1 jit_solution(4211785401332058846)
XLA Ops:
  0.6 40.5 %shard_map.131 = (bf16[128,1024]{1,0:T(8,128)(2,1)S(1)}, bf16[128,2048]{1,0:T(8,128)(2,1)S(1)}, f32[1,2048]{1,0:T(1,128)S(1)}) custom-call(bf16[128,1024]{1,0:T(8,128)(2,1)} %q_in.1, bf16[128,256]{1,0:T(8,128)(2,1)} %k_in.1, bf16[128,256]{1,0:T(8,128)(2,1)} %v_in.1, bf16[128,2048]{1,0:T(8,128)(2,1)} %x_in.1, bf16[128,2048]{1,0:T(8,128)(2,1)} %z_in.1, ...), custom_call_target="tpu_custom_call" | custom-call | tf_op jit(solution)/shard_map/pallas_call | solution.py:685
  41.1 1.0 %shard_map.132 = (bf16[128,1024]{1,0:T(8,128)(2,1)}, bf16[128,2048]{1,0:T(8,128)(2,1)}) custom-call(bf16[128,1024]{1,0:T(8,128)(2,1)S(1)} %get-tuple-element.5.ctx_ref, bf16[128,2048]{1,0:T(8,128)(2,1)S(1)} %get-tuple-element.6.gated_ref, f32[1,2048]{1,0:T(1,128)S(1)} %get-tuple-element.7.gain_ref), custom_call_target="tpu_custom_call" | custom-call | tf_op jit(solution)/shard_map/pallas_call | solution.py:748

commit v6 on v5

--- a/solution.py
+++ b/solution.py
@@ -42,7 +42,7 @@
     kv_all, bias_scr, ctx_stage, gated, base_scr, er_scr, xdt_scr, hs, run_split, gmask,
     buf_a, buf_b, out_a, out_b, sloc_a, sloc_b, tot_a, tot_b, log_in, log_out, wide_t,
     kv_plus, kv_minus, kv_recv, a_send, a_recv, b_send, b_recv, o_send, o_recv, c_send, c_recv,
-    log_send, log_recv, plus_sem, minus_sem, pair_plus, pair_minus, load_sem,
+    log_send, log_recv, q_more, ctx_more, q_send, q_recv, m_send, plus_sem, minus_sem, pair_plus, pair_minus, load_sem,
 ):
     me = lax.axis_index("ctx")
     tok = q_ref.shape[0]
@@ -66,6 +66,9 @@
     partner = core + 1 - 2 * lax.rem(core, 2)
     has_left = me > 0
     has_right = me < n - 1
+    helped = (me == n - 1) & (n > 1)
+    helper = (me == n - 2) & (n > 1)
+    kv_right_on = me < n - 2
 
     b_ref, c_ref = bc_ref.at[0], bc_ref.at[1]
     bias_ref, alog_ref, skip_ref = (small_ref.at[i] for i in range(3))
@@ -159,12 +162,14 @@
     target = lax.broadcasted_iota(jnp.int32, (half, lanes), 0)
     causal = source <= target
     diagonal = source == target
-    for g in range(groups):
-        cols = slice(g * MN, (g + 1) * MN)
-        for which in range(2):
-            rows = slice(which * half, (which + 1) * half)
-            repeated = jnp.concatenate([b_ref[rows, cols]] * per_unit, axis=0)
-            gmask[g, rows, :] = jnp.where(causal, dot(c_ref[rows, cols], repeated, 1, 1), 0.0)
+
+    def causal_products():
+        for g in range(groups):
+            cols = slice(g * MN, (g + 1) * MN)
+            for which in range(2):
+                rows = slice(which * half, (which + 1) * half)
+                repeated = jnp.concatenate([b_ref[rows, cols]] * per_unit, axis=0)
+                gmask[g, rows, :] = jnp.where(causal, dot(c_ref[rows, cols], repeated, 1, 1), 0.0)
 
     @pl.when(me == 0)
     def _():
@@ -184,9 +189,10 @@
     def block_id(which):
         return me if which == 0 else 2 * n - 1 - me
 
-    def send(stage, final, cols, send_sem, recv_sem, which):
-        owner = block_id(which) // 2
-        slot = lax.rem(block_id(which), 2)
+    def send(stage, final, cols, send_sem, recv_sem, which, block=None):
+        block = block_id(which) if block is None else block
+        owner = block // 2
+        slot = lax.rem(block, 2)
         rows = pl.ds(which * half, half)
         target = pl.ds(pl.multiple_of(slot * half, half), half)
 
@@ -313,9 +319,12 @@
         def _():
             kv_right(source).wait_recv()
 
-        @pl.when(has_right)
+        @pl.when(kv_right_on)
         def _():
             kv_right(source).start()
+
+    def q_copy():
+        return remote(q_ref, q_more, q_send, q_recv, jnp.maximum(me - 1, 0))
 
     def relay_left(h):
         source = jnp.minimum(me + h, n - 1)
@@ -328,7 +337,7 @@
             def _(copy=copy):
                 copy.start()
 
-    def attention_mask():
+    def attention_mask(who):
         def clear(s, _):
             @pl.when(s < me)
             def _():
@@ -344,21 +353,21 @@
             within < half, source * half + within, (2 * n - 2 - source) * half + within
         )
         query = lax.broadcasted_iota(jnp.int32, (tok, n * tok), 0)
-        query_pos = jnp.where(query < half, me * half + query, (2 * n - 2 - me) * half + query)
+        query_pos = jnp.where(query < half, who * half + query, (2 * n - 2 - who) * half + query)
         bias_scr[...] = jnp.where(key_pos <= query_pos, 0.0, MASKED)
 
     scale = 1.0 / math.sqrt(HEAD_SIZE)
 
-    def one_head(h):
+    def one_head(h, queries, stage):
         hcols = pl.ds(pl.multiple_of(h * HEAD_SIZE, HEAD_SIZE), HEAD_SIZE)
         kcols = pl.ds(pl.multiple_of((h // repeat) * HEAD_SIZE, HEAD_SIZE), HEAD_SIZE)
         vcols = pl.ds(pl.multiple_of(kv + (h // repeat) * HEAD_SIZE, HEAD_SIZE), HEAD_SIZE)
         keys = kv_all[:, :, kcols].reshape(n * tok, HEAD_SIZE)
         values = kv_all[:, :, vcols].reshape(n * tok, HEAD_SIZE)
-        scores = dot(q_ref[:, hcols], keys, 1, 1) * scale + bias_scr[...]
+        scores = dot(queries[:, hcols], keys, 1, 1) * scale + bias_scr[...]
         expo = jnp.exp(scores - jnp.max(scores, axis=-1, keepdims=True))
         total = jnp.sum(expo, axis=-1, keepdims=True)
-        ctx_stage[:, hcols] = (dot(expo.astype(BF16), values) / total).astype(BF16)
+        stage[:, hcols] = (dot(expo.astype(BF16), values) / total).astype(BF16)
 
     def send_ctx():
         for which in range(2):
@@ -381,10 +390,13 @@
 
     @pl.when(has_right & has_left)
     def _():
-        kv_right(me).start()
         for copy in kv_left(me):
             copy.start()
 
+    @pl.when(kv_right_on & has_left)
+    def _():
+        kv_right(me).start()
+
     prepare(0)
 
     @pl.when(jnp.logical_not(has_left))
@@ -395,10 +407,6 @@
         @pl.when(k > 0)
         def _():
             prepare(k)
-
-        @pl.when((k == units // 2) & (me == 0))
-        def _():
-            relay_right(0)
 
         @pl.when((k == units // 2) & (me == n - 1))
         def _():
@@ -415,10 +423,18 @@
 
         return 0
 
-    lax.fori_loop(0, units, first_step, 0)
+    between = has_left & has_right
+    lax.fori_loop(0, jnp.where(between, units - 2, units), first_step, 0)
     for load in loads[5:7]:
         load.wait()
-    attention_mask()
+
+    @pl.when((me == 0) & kv_right_on)
+    def _():
+        relay_right(0)
+
+    @pl.when(helped)
+    def _():
+        q_copy().start()
 
     def base(distance):
         return (14 * jnp.maximum(distance - 1, 0)) // 3
@@ -429,8 +445,8 @@
     hold_plus = block_b // 2 - 1 > me
     hold_minus = me // 2 + 1 < me
     gap = jnp.where(hops > 1, 6, 2)
-    free = jnp.maximum(lag_a + pieces + 1, lag_b + pieces + gap + 1)
-    gates = jnp.maximum(lag_a, lag_b + gap) + pieces - units + 3
+    free = jnp.maximum(lag_a + pieces - 1, lag_b + pieces + gap + 1)
+    gates = jnp.maximum(lag_a - 2, lag_b + gap) + pieces - units + 3
     gates = gates + jnp.where(2 * me < n, jnp.where(has_left, 3, 0), jnp.where(has_right, 7, 1))
     gates = jnp.maximum(gates, jnp.where(hold_plus, lag_a + pieces + 2, 0))
     gates = jnp.maximum(gates, jnp.where(hold_minus, lag_b + pieces + gap + 2, 0))
@@ -469,17 +485,15 @@
     def chain_a(t):
         at = t - lag_a
 
-        @pl.when((at == middle) & has_left)
+        @pl.when((at >= 0) & (at < pieces) & has_left)
+        def _():
+            step_a(at)
+
+        @pl.when((at == pieces + 1) & has_left & kv_right_on)
         def _():
             relay_right(me)
 
-        k = jnp.where(at < middle, at, at - 2)
-
-        @pl.when(((at >= 0) & (at < middle) | (at > middle + 1) & (at < pieces + 2)) & has_left)
-        def _():
-            step_a(k)
-
-        @pl.when((at == pieces + 1) & has_left)
+        @pl.when((at == pieces - 1) & has_left)
         def _():
             greet_pair(pair_plus, plus_peers)
 
@@ -521,13 +535,21 @@
             release(pair_plus, plus_sem, plus_peers)
 
         for h in range(1, n - 1):
-            @pl.when((t == 4 * h - 4) & (h < me))
+            @pl.when((t == 4 * h - 4) & (h < me) & jnp.logical_not(helped))
             def _(h=h):
                 relay_right(h)
 
             @pl.when((t == 6 * h - 4) & (h < hops))
             def _(h=h):
                 relay_left(h)
+
+        @pl.when(t == 0)
+        def _():
+            causal_products()
+
+        @pl.when(between & ((t == 1) | (t == 3)))
+        def _():
+            prepare(units - 2 + t // 2)
 
         @pl.when((t < 2 * units) & (lax.rem(t, 2) == 0))
         def _():
@@ -593,13 +615,31 @@
 
             lax.fori_loop(0, units, send_rest, 0)
 
-    def two_heads(i, _):
-        one_head(2 * i)
-        one_head(2 * i + 1)
-        return 0
-
-    lax.fori_loop(0, q_heads // 2, two_heads, 0)
-    send_ctx()
+    def attend(who, queries, stage):
+        attention_mask(who)
+
+        def two_heads(i, _):
+            one_head(2 * i, queries, stage)
+            one_head(2 * i + 1, queries, stage)
+            return 0
+
+        lax.fori_loop(0, q_heads // 2, two_heads, 0)
+
+    @pl.when(helper & has_left)
+    def _():
+        kv_right(0).wait_recv()
+
+    @pl.when(jnp.logical_not(helped))
+    def _():
+        attend(me, q_ref, ctx_stage)
+        send_ctx()
+
+    @pl.when(helper)
+    def _():
+        q_copy().wait_recv()
+        attend(n - 1, q_more, ctx_more)
+        for which in range(2):
+            send(ctx_more, ctx_out, slice(None), m_send, c_recv, which, jnp.int32(n - 1 + which))
 
     @pl.when(has_right)
     def _():
@@ -614,7 +654,7 @@
         log_copy().wait_send()
 
     for i in range(n):
-        @pl.when((me == i) & has_right)
+        @pl.when((me == i) & kv_right_on)
         def _(i=i):
             part = kv_all.at[pl.ds(0, i + 1), first]
             remote(part, part, kv_plus, kv_recv.at[0, 0], me).wait_send()
@@ -624,23 +664,40 @@
             part = kv_all.at[pl.ds(i, n - i)]
             remote(part, part, kv_minus, kv_recv.at[0, 0], me).wait_send()
 
-    def settle(stage, final, send_sem, recv_sem):
-        def whole(rows):
-            return remote(stage.at[pl.ds(0, rows)], final.at[pl.ds(0, rows)], send_sem, recv_sem, me)
-
-        kept = (block_id(0) // 2 == me) | (block_id(1) // 2 == me)
-        for rows, here in ((tok, jnp.logical_not(kept)), (half, kept)):
-            @pl.when(here)
-            def _(rows=rows):
-                whole(rows).wait_send()
-
-            @pl.when(here)
-            def _(rows=rows):
-                whole(rows).wait_recv()
-
-    settle(ctx_stage, ctx_out, c_send, c_recv)
+    def settle(stage, final, send_sem, recv_sem, away, missing):
+        for count in (1, 2):
+            rows = pl.ds(0, count * half)
+            copy = remote(stage.at[rows], final.at[rows], send_sem, recv_sem, me)
+
+            @pl.when(away == count)
+            def _(copy=copy):
+                copy.wait_send()
+
+            @pl.when(missing == count)
+            def _(copy=copy):
+                copy.wait_recv()
+
+    def tally(flags):
+        return sum(jnp.where(flag, 1, 0) for flag in flags)
+
+    def source_of(slot):
+        block = 2 * me + slot
+        return jnp.where(block < n, block, 2 * n - 1 - block)
+
+    away = tally(block_id(which) // 2 != me for which in range(2))
+    missing = tally(source_of(slot) != me for slot in range(2))
+    served = [jnp.minimum(source_of(slot), n - 2) if n > 1 else source_of(slot) for slot in range(2)]
+    served_missing = tally(source != me for source in served)
+    more = sum(1 for block in (n - 1, n) if block // 2 != n - 2)
+
+    @pl.when(helped)
+    def _():
+        q_copy().wait_send()
+
+    settle(ctx_stage, ctx_out, c_send, c_recv, jnp.where(helped, 0, away), served_missing)
+    settle(ctx_more, ctx_out, m_send, c_recv, jnp.where(helper, more, 0), 0)
     loads[7].wait()
-    settle(gated, arrived, o_send, o_recv)
+    settle(gated, arrived, o_send, o_recv, away, missing)
 
 
 def finish(groups, ctx_ref, gated_ref, gain_ref, ctx_out, mix_out, mixed, sems):
@@ -732,6 +789,11 @@
             dma(()),
             dma(()),
             dma(()),
+            vmem(query.shape, BF16),
+            vmem(query.shape, BF16),
+            dma(()),
+            dma(()),
+            dma(()),
             pltpu.SemaphoreType.REGULAR,
             pltpu.SemaphoreType.REGULAR,
             pltpu.SemaphoreType.REGULAR,

time: 42.3 us -> 41.5 us (0.981)
  Pallas kernels: 41.4 us -> 40.7 us
    pallas_call x1, Pallas kernels: 40.5 us -> 39.7 us  [body(): pl.pallas_call(functools.partial(kernel, n, wide_hd), out_shape=(vmem(que...]
where the time goes in v6:
time: 41.5 us; the launch traced here: 41.3 us
  Pallas kernels  40.7 us (98%)
  between operations  0.64 us (2%)
    pallas_call x1, Pallas kernels, body(): pl.pallas_call(functools.partial(kernel, n, wide_hd), out_shape=(vmem(que...  39.7 us
    pallas_call x1, Pallas kernels, body(): pl.pallas_call(functools.partial(finish, groups), out_shape=(jax.ShapeDty...  0.96 us

profile of v6, /device:TPU:26, one launch (start us, length us, event | category | flops | bytes accessed | tf_op | source)
XLA Modules:
  0.0 41.3 jit_solution(10944483650491358146)
XLA Ops:
  0.6 39.7 %shard_map.131 = (bf16[128,1024]{1,0:T(8,128)(2,1)S(1)}, bf16[128,2048]{1,0:T(8,128)(2,1)S(1)}, f32[1,2048]{1,0:T(1,128)S(1)}) custom-call(bf16[128,1024]{1,0:T(8,128)(2,1)} %q_in.1, bf16[128,256]{1,0:T(8,128)(2,1)} %k_in.1, bf16[128,256]{1,0:T(8,128)(2,1)} %v_in.1, bf16[128,2048]{1,0:T(8,128)(2,1)} %x_in.1, bf16[128,2048]{1,0:T(8,128)(2,1)} %z_in.1, ...), custom_call_target="tpu_custom_call" | custom-call | tf_op jit(solution)/shard_map/pallas_call | solution.py:742
  40.4 1.0 %shard_map.132 = (bf16[128,1024]{1,0:T(8,128)(2,1)}, bf16[128,2048]{1,0:T(8,128)(2,1)}) custom-call(bf16[128,1024]{1,0:T(8,128)(2,1)S(1)} %get-tuple-element.5.ctx_ref, bf16[128,2048]{1,0:T(8,128)(2,1)S(1)} %get-tuple-element.6.gated_ref, f32[1,2048]{1,0:T(1,128)S(1)} %get-tuple-element.7.gain_ref), custom_call_target="tpu_custom_call" | custom-call | tf_op jit(solution)/shard_map/pallas_call | solution.py:810

commit v7 on v6

--- a/solution.py
+++ b/solution.py
@@ -447,7 +447,7 @@
     gap = jnp.where(hops > 1, 6, 2)
     free = jnp.maximum(lag_a + pieces - 1, lag_b + pieces + gap + 1)
     gates = jnp.maximum(lag_a - 2, lag_b + gap) + pieces - units + 3
-    gates = gates + jnp.where(2 * me < n, jnp.where(has_left, 3, 0), jnp.where(has_right, 7, 1))
+    gates = gates + jnp.where(2 * me < n, jnp.where(has_left, 1, 0), jnp.where(has_right, 7, 1))
     gates = jnp.maximum(gates, jnp.where(hold_plus, lag_a + pieces + 2, 0))
     gates = jnp.maximum(gates, jnp.where(hold_minus, lag_b + pieces + gap + 2, 0))
     quick = gates >= jnp.maximum(lag_a + pieces + 2, lag_b + pieces + gap + 2)
@@ -493,7 +493,7 @@
         def _():
             relay_right(me)
 
-        @pl.when((at == pieces - 1) & has_left)
+        @pl.when((at == pieces - 3) & has_left)
         def _():
             greet_pair(pair_plus, plus_peers)
 
@@ -529,10 +529,13 @@
         def _():
             chain_b(t)
 
+        @pl.when(t == lag_a + pieces - 2)
+        def _():
+            release(pair_plus, plus_sem, plus_peers)
+
         @pl.when(t == free)
         def _():
             release(pair_minus, minus_sem, minus_peers)
-            release(pair_plus, plus_sem, plus_peers)
 
         for h in range(1, n - 1):
             @pl.when((t == 4 * h - 4) & (h < me) & jnp.logical_not(helped))

time: 41.5 us -> 41.2 us (level)
  Pallas kernels: 40.7 us -> 40 us
    pallas_call x1, Pallas kernels: 39.7 us -> 39 us  [body(): pl.pallas_call(functools.partial(kernel, n, wide_hd), out_shape=(vmem(que...]
where the time goes in v7:
time: 41.2 us; the launch traced here: 40.6 us
  Pallas kernels  40 us (97%)
  between operations  0.64 us (2%)
    pallas_call x1, Pallas kernels, body(): pl.pallas_call(functools.partial(kernel, n, wide_hd), out_shape=(vmem(que...  39 us
    pallas_call x1, Pallas kernels, body(): pl.pallas_call(functools.partial(finish, groups), out_shape=(jax.ShapeDty...  0.96 us

profile of v7, /device:TPU:26, one launch (start us, length us, event | category | flops | bytes accessed | tf_op | source)
XLA Modules:
  0.0 40.6 jit_solution(15901253788769968482)
XLA Ops:
  0.6 39.0 %shard_map.131 = (bf16[128,1024]{1,0:T(8,128)(2,1)S(1)}, bf16[128,2048]{1,0:T(8,128)(2,1)S(1)}, f32[1,2048]{1,0:T(1,128)S(1)}) custom-call(bf16[128,1024]{1,0:T(8,128)(2,1)} %q_in.1, bf16[128,256]{1,0:T(8,128)(2,1)} %k_in.1, bf16[128,256]{1,0:T(8,128)(2,1)} %v_in.1, bf16[128,2048]{1,0:T(8,128)(2,1)} %x_in.1, bf16[128,2048]{1,0:T(8,128)(2,1)} %z_in.1, ...), custom_call_target="tpu_custom_call" | custom-call | tf_op jit(solution)/shard_map/pallas_call | solution.py:745
  39.7 1.0 %shard_map.132 = (bf16[128,1024]{1,0:T(8,128)(2,1)}, bf16[128,2048]{1,0:T(8,128)(2,1)}) custom-call(bf16[128,1024]{1,0:T(8,128)(2,1)S(1)} %get-tuple-element.5.ctx_ref, bf16[128,2048]{1,0:T(8,128)(2,1)S(1)} %get-tuple-element.6.gated_ref, f32[1,2048]{1,0:T(1,128)S(1)} %get-tuple-element.7.gain_ref), custom_call_target="tpu_custom_call" | custom-call | tf_op jit(solution)/shard_map/pallas_call | solution.py:813

commit v8 on v7

--- a/solution.py
+++ b/solution.py
@@ -453,7 +453,7 @@
     quick = gates >= jnp.maximum(lag_a + pieces + 2, lag_b + pieces + gap + 2)
     ending = has_left & jnp.logical_not(has_right)
     first_out = jnp.where((2 * me < n) | jnp.logical_not(has_right), 1, 0)
-    early = lag_b + middle + 1
+    early = lag_b + middle
     fills = has_left & has_right & (2 * me >= n) & (lag_a + 2 * span <= early)
     last = functools.reduce(jnp.maximum, [
         lag_a + pieces + 2, lag_b + pieces + gap + 2, gates + jnp.where(quick, middle // 2, middle),

time: 41.2 us -> 41.2 us (level)
  no operation moved by 1% of the time
where the time goes in v8:
time: 41.2 us; the launch traced here: 40.6 us
  Pallas kernels  40 us (97%)
  between operations  0.64 us (2%)
    pallas_call x1, Pallas kernels, body(): pl.pallas_call(functools.partial(kernel, n, wide_hd), out_shape=(vmem(que...  39 us
    pallas_call x1, Pallas kernels, body(): pl.pallas_call(functools.partial(finish, groups), out_shape=(jax.ShapeDty...  0.96 us

profile of v8, /device:TPU:26, one launch (start us, length us, event | category | flops | bytes accessed | tf_op | source)
XLA Modules:
  0.0 40.6 jit_solution(1136134489635648035)
XLA Ops:
  0.6 39.0 %shard_map.131 = (bf16[128,1024]{1,0:T(8,128)(2,1)S(1)}, bf16[128,2048]{1,0:T(8,128)(2,1)S(1)}, f32[1,2048]{1,0:T(1,128)S(1)}) custom-call(bf16[128,1024]{1,0:T(8,128)(2,1)} %q_in.1, bf16[128,256]{1,0:T(8,128)(2,1)} %k_in.1, bf16[128,256]{1,0:T(8,128)(2,1)} %v_in.1, bf16[128,2048]{1,0:T(8,128)(2,1)} %x_in.1, bf16[128,2048]{1,0:T(8,128)(2,1)} %z_in.1, ...), custom_call_target="tpu_custom_call" | custom-call | tf_op jit(solution)/shard_map/pallas_call | solution.py:745
  39.7 1.0 %shard_map.132 = (bf16[128,1024]{1,0:T(8,128)(2,1)}, bf16[128,2048]{1,0:T(8,128)(2,1)}) custom-call(bf16[128,1024]{1,0:T(8,128)(2,1)S(1)} %get-tuple-element.5.ctx_ref, bf16[128,2048]{1,0:T(8,128)(2,1)S(1)} %get-tuple-element.6.gated_ref, f32[1,2048]{1,0:T(1,128)S(1)} %get-tuple-element.7.gain_ref), custom_call_target="tpu_custom_call" | custom-call | tf_op jit(solution)/shard_map/pallas_call | solution.py:813

commit v9 on v8

--- a/solution.py
+++ b/solution.py
@@ -450,7 +450,7 @@
     gates = gates + jnp.where(2 * me < n, jnp.where(has_left, 1, 0), jnp.where(has_right, 7, 1))
     gates = jnp.maximum(gates, jnp.where(hold_plus, lag_a + pieces + 2, 0))
     gates = jnp.maximum(gates, jnp.where(hold_minus, lag_b + pieces + gap + 2, 0))
-    quick = gates >= jnp.maximum(lag_a + pieces + 2, lag_b + pieces + gap + 2)
+    quick = gates >= jnp.maximum(lag_a + pieces, lag_b + pieces + gap + 2)
     ending = has_left & jnp.logical_not(has_right)
     first_out = jnp.where((2 * me < n) | jnp.logical_not(has_right), 1, 0)
     early = lag_b + middle

time: 41.2 us -> 41 us (level)
  no operation moved by 1% of the time
where the time goes in v9:
time: 41 us; the launch traced here: 40.6 us
  Pallas kernels  40 us (98%)
  between operations  0.64 us (2%)
    pallas_call x1, Pallas kernels, body(): pl.pallas_call(functools.partial(kernel, n, wide_hd), out_shape=(vmem(que...  39 us
    pallas_call x1, Pallas kernels, body(): pl.pallas_call(functools.partial(finish, groups), out_shape=(jax.ShapeDty...  0.96 us

profile of v9, /device:TPU:26, one launch (start us, length us, event | category | flops | bytes accessed | tf_op | source)
XLA Modules:
  0.0 40.6 jit_solution(2873218786106806641)
XLA Ops:
  0.6 39.0 %shard_map.131 = (bf16[128,1024]{1,0:T(8,128)(2,1)S(1)}, bf16[128,2048]{1,0:T(8,128)(2,1)S(1)}, f32[1,2048]{1,0:T(1,128)S(1)}) custom-call(bf16[128,1024]{1,0:T(8,128)(2,1)} %q_in.1, bf16[128,256]{1,0:T(8,128)(2,1)} %k_in.1, bf16[128,256]{1,0:T(8,128)(2,1)} %v_in.1, bf16[128,2048]{1,0:T(8,128)(2,1)} %x_in.1, bf16[128,2048]{1,0:T(8,128)(2,1)} %z_in.1, ...), custom_call_target="tpu_custom_call" | custom-call | tf_op jit(solution)/shard_map/pallas_call | solution.py:745
  39.7 1.0 %shard_map.132 = (bf16[128,1024]{1,0:T(8,128)(2,1)}, bf16[128,2048]{1,0:T(8,128)(2,1)}) custom-call(bf16[128,1024]{1,0:T(8,128)(2,1)S(1)} %get-tuple-element.5.ctx_ref, bf16[128,2048]{1,0:T(8,128)(2,1)S(1)} %get-tuple-element.6.gated_ref, f32[1,2048]{1,0:T(1,128)S(1)} %get-tuple-element.7.gain_ref), custom_call_target="tpu_custom_call" | custom-call | tf_op jit(solution)/shard_map/pallas_call | solution.py:813
